TPU v7x, 32 devices: a whole 2x2x4 slice. The times are simulated.
32 devices in a mesh: fsdp: 32 (over z, y, x, core).
Axes of the slice: x: 2, y: 2, z: 4, core: 2. Of those that a mesh axis runs over, the one named last changes fastest.
Arguments:
- tokens: int32 [32, 256], P('fsdp')
- embed_table: float32 [32000, 2048], P('fsdp')
- norm_gain: float32 [2048], P('fsdp')
- w_query: float32 [2048, 2048], P('fsdp')
- w_key: float32 [2048, 2048], P('fsdp')
- w_value: float32 [2048, 2048], P('fsdp')
- d_query: bfloat16 [32, 256, 2048], P('fsdp')
- d_key: bfloat16 [32, 256, 2048], P('fsdp')
- d_value: bfloat16 [32, 256, 2048], P('fsdp')
Outputs:
- output 1: bfloat16 [32, 256, 2048], P('fsdp')
- output 2: bfloat16 [32, 256, 2048], P('fsdp')
- output 3: bfloat16 [32, 256, 2048], P('fsdp')
- output 4: float32 [32000, 2048], P('fsdp')
- output 5: float32 [2048], P('fsdp')
- output 6: float32 [2048, 2048], P('fsdp')
- output 7: float32 [2048, 2048], P('fsdp')
- output 8: float32 [2048, 2048], P('fsdp')
All inputs are finite; a program needn't handle non-finite values.
Results may differ from a plain program's by a relative error of at most 0.00413151.
Values are sent between devices in bfloat16 or wider.
A program may use at most 1 GiB of HBM per device.

v0:
```python
import jax
import jax.numpy as jnp
from jax import lax
from jax.sharding import PartitionSpec as P

AXIS_NAME = "fsdp"


def norm_forward(x_rows, gain_full):
    inv_rms = lax.rsqrt(jnp.mean(x_rows * x_rows, axis=-1, keepdims=True) + 1e-5)
    h_rows = x_rows * inv_rms
    return inv_rms, h_rows, (h_rows * gain_full).astype(jnp.bfloat16)


def solution(mesh):
    def local_step(tokens, embed_shard, gain_shard, wq_shard, wk_shard, wv_shard, d_query, d_key, d_value):
        vocab_local = embed_shard.shape[0]
        dev_index = lax.axis_index(AXIS_NAME)
        all_tokens = lax.all_gather(tokens, AXIS_NAME, axis=0, tiled=True)
        local_ids = all_tokens - dev_index * vocab_local
        is_owned = (local_ids >= 0) & (local_ids < vocab_local)
        owned_rows = jnp.take(embed_shard, jnp.where(is_owned, local_ids, 0), axis=0).astype(jnp.bfloat16)
        part_rows = jnp.where(is_owned[:, :, None], owned_rows, jnp.zeros((), jnp.bfloat16))
        x_rows = lax.psum_scatter(part_rows, AXIS_NAME, scatter_dimension=0, tiled=True).astype(jnp.float32)
        gain_full = lax.all_gather(gain_shard, AXIS_NAME, axis=0, tiled=True)
        wq_full = lax.all_gather(wq_shard.astype(jnp.bfloat16), AXIS_NAME, axis=0, tiled=True)
        wk_full = lax.all_gather(wk_shard.astype(jnp.bfloat16), AXIS_NAME, axis=0, tiled=True)
        wv_full = lax.all_gather(wv_shard.astype(jnp.bfloat16), AXIS_NAME, axis=0, tiled=True)
        inv_rms, h_rows, normed = norm_forward(x_rows, gain_full)
        query_proj = jnp.einsum("bsd,df->bsf", normed, wq_full, preferred_element_type=jnp.float32).astype(jnp.bfloat16)
        key_proj = jnp.einsum("bsd,df->bsf", normed, wk_full, preferred_element_type=jnp.float32).astype(jnp.bfloat16)
        value_proj = jnp.einsum("bsd,df->bsf", normed, wv_full, preferred_element_type=jnp.float32).astype(jnp.bfloat16)
        d_w_query = lax.psum_scatter(jnp.einsum("bsd,bsf->df", normed, d_query, preferred_element_type=jnp.float32), AXIS_NAME, scatter_dimension=0, tiled=True)
        d_w_key = lax.psum_scatter(jnp.einsum("bsd,bsf->df", normed, d_key, preferred_element_type=jnp.float32), AXIS_NAME, scatter_dimension=0, tiled=True)
        d_w_value = lax.psum_scatter(jnp.einsum("bsd,bsf->df", normed, d_value, preferred_element_type=jnp.float32), AXIS_NAME, scatter_dimension=0, tiled=True)
        d_normed = (jnp.einsum("bsf,df->bsd", d_query, wq_full, preferred_element_type=jnp.float32)
                    + jnp.einsum("bsf,df->bsd", d_key, wk_full, preferred_element_type=jnp.float32)
                    + jnp.einsum("bsf,df->bsd", d_value, wv_full, preferred_element_type=jnp.float32))
        d_norm_gain = lax.psum_scatter(jnp.sum(d_normed * h_rows, axis=(0, 1)), AXIS_NAME, scatter_dimension=0, tiled=True)
        u_rows = d_normed * gain_full
        d_x = inv_rms * (u_rows - h_rows * jnp.mean(u_rows * h_rows, axis=-1, keepdims=True))
        all_dx = lax.all_gather(d_x, AXIS_NAME, axis=0, tiled=True)
        scatter_ids = jnp.where(is_owned, local_ids, vocab_local)
        d_embed = jnp.zeros(embed_shard.shape, jnp.float32).at[scatter_ids].add(all_dx, mode="drop")
        return (query_proj, key_proj, value_proj, d_embed, d_norm_gain, d_w_query, d_w_key, d_w_value)

    row_spec = P(AXIS_NAME, None)
    act_spec = P(AXIS_NAME, None, None)
    vec_spec = P(AXIS_NAME)
    return jax.shard_map(local_step, mesh=mesh,
                         in_specs=(row_spec, row_spec, vec_spec, row_spec, row_spec, row_spec, act_spec, act_spec, act_spec),
                         out_specs=(act_spec, act_spec, act_spec, row_spec, vec_spec, row_spec, row_spec, row_spec),
                         check_vma=False)
```

profile of v0, /device:TPU:14, one launch (start us, length us, event | category | flops | bytes accessed | tf_op | source)
XLA Modules:
  0.0 1546.2 jit_solution(13025440376103058266)
XLA Ops:
  7.2 0.0 all-gather.6.cloned.1.call-start
  7.2 1.8 convert_element_type.39
  9.1 0.0 all-gather.6.cloned.1.call-update
  9.1 0.0 all-gather.8.cloned.1.call-start
  9.2 1.8 convert_element_type.42
  10.9 0.0 all-gather.8.cloned.1.call-update
  11.0 0.0 reduce-scatter.5.cloned.1.call-start
  11.0 28.9 %all-gather = s32[32,1,256]{2,1,0:T(1,128)S(1)} all-gather(s32[1,1,256]{2,1,0:T(1,128)S(1)} %bitcast.82), channel_id=1, replica_groups=mesh['fsdp'=32] {'fsdp'}, dimensions={0}, use_global_device_ids=true | all-gather | bytes 33792 | tf_op jit(solution)/shard_map/all_gather | solution.py:19
  40.0 0.6 fusion.27
  40.6 64.7 %gather_fusion = bf16[8192,2048]{1,0:T(8,128)(2,1)} fusion(f32[1000,2048]{1,0:T(8,128)} %param.10, s32[8192]{0:T(1024)S(1)} %broadcast_clamp_fusion), kind=kCustom, calls=%fused_computation | custom fusion | bytes 67141632 | tf_op jit(solution)/shard_map/jit(_take)/gather | solution.py:22
  105.3 22.8 %fusion = bf16[32,256,2048]{2,1,0:T(8,128)(2,1)} fusion(bf16[32,256,2048]{2,1,0:T(8,128)(2,1)} %bitcast.76, pred[32,256]{1,0:T(8,128)(4,1)S(1)} %get-tuple-element.13, pred[32,256]{1,0:T(8,128)(4,1)S(1)} %get-tuple-element.12), kind=kLoop, calls=%fused_computation.3 | loop fusion | flops 33554432 | bytes 67125248 | tf_op jit(solution)/shard_map/jit(_where)/select_n | solution.py:23
  128.1 0.0 reduce-scatter.5.cloned.1.call-update
  128.2 0.0 all-gather.10.cloned.1.call-start
  128.2 0.9 copy-done.5
  129.2 0.7 convert_element_type.45
  129.9 0.0 all-gather.10.cloned.1.call-update
  129.9 0.0 all-gather.12.cloned.1.call-start
  130.0 0.3 dynamic-update-slice
  130.3 68.7 %all-reduce = f32[2048]{0:T(1024)S(1)} all-reduce(f32[2048]{0:T(1024)S(1)} %dynamic-update-slice), channel_id=1, replica_groups=mesh['fsdp'=32] {'fsdp'}, use_global_device_ids=true, to_apply=%add | all-reduce | flops 2048 | bytes 16384
  199.0 7.3 fusion.25
  206.3 7.7 convolution_add_fusion.1
  214.0 318.7 %reduce-scatter.5.cloned.1.call-done = bf16[1,256,2048]{2,1,0:T(8,128)(2,1)} async-done(((bf16[32,256,2048]{2,1,0:T(8,128)(2,1)}), bf16[1,256,2048]{2,1,0:T(8,128)(2,1)}) %reduce-scatter.5.cloned.1.call-update) | async-done | bytes 1048592 | tf_op jit(solution)/shard_map/reduce_scatter | solution.py:24
  532.7 1.5 fusion.15
  534.2 78.6 %all-gather.10.cloned.1.call-done = bf16[2048,2048]{1,0:T(8,128)(2,1)} async-done(((bf16[64,2048]{1,0:T(8,128)(2,1)}), bf16[2048,2048]{1,0:T(8,128)(2,1)}) %all-gather.10.cloned.1.call-update) | async-done | bytes 8388624 | tf_op jit(solution)/shard_map/all_gather | solution.py:28
  612.8 7.1 fusion.14
  619.9 1.8 fusion.13
  621.7 0.0 all-gather.12.cloned.1.call-update
  621.7 0.2 reduce-scatter.7.cloned.1.call-start
  622.0 8.3 fusion.23
  630.3 0.0 reduce-scatter.7.cloned.1.call-update
  630.3 0.0 reduce-scatter.9.cloned.1.call-start
  630.4 1.2 copy-done.4
  631.5 8.3 fusion.20
  639.8 0.0 reduce-scatter.9.cloned.1.call-update
  639.9 0.0 reduce-scatter.11.cloned.1.call-start
  639.9 8.2 fusion.17
  648.1 0.0 reduce-scatter.11.cloned.1.call-update
  648.1 0.7 copy-done.6
  648.9 42.1 %all-reduce.1 = f32[2048]{0:T(1024)S(1)} all-reduce(f32[2048]{0:T(1024)S(1)} %get-tuple-element.8), channel_id=3, replica_groups=mesh['fsdp'=32] {'fsdp'}, use_global_device_ids=true, to_apply=%region_5.6.clone | all-reduce | flops 2048 | bytes 16384
  690.9 0.6 dynamic-slice
  691.5 6.9 fusion.7
  698.4 6.9 fusion.8
  705.4 3.4 fusion.9
  708.7 266.3 %all-gather.12.cloned.1.call-done = f32[32,256,2048]{2,1,0:T(8,128)} async-done(((f32[1,256,2048]{2,1,0:T(8,128)}), f32[32,256,2048]{2,1,0:T(8,128)}) %all-gather.12.cloned.1.call-update) | async-done | bytes 67108880 | tf_op jit(solution)/shard_map/all_gather | solution.py:42
  975.1 105.9 %scatter_custom_fusion = f32[1000,2048]{1,0:T(8,128)} fusion(s32[8192]{0:T(1024)S(1)} %bitcast.81, f32[8192,2048]{1,0:T(8,128)} %bitcast.10, f32[]{:T(128)} %constant.15.clone.1), kind=kCustom, calls=%fused_computation.4 | custom fusion | flops 16777216 | bytes 8192512 | tf_op jit(solution)/shard_map/scatter-add | solution.py:44
  1081.0 83.5 %reduce-scatter.7.cloned.1.call-done = f32[64,2048]{1,0:T(8,128)} async-done(((f32[2048,2048]{1,0:T(8,128)}), f32[64,2048]{1,0:T(8,128)}) %reduce-scatter.7.cloned.1.call-update) | async-done | bytes 524304 | tf_op jit(solution)/shard_map/reduce_scatter | solution.py:33
  1164.5 187.4 %reduce-scatter.9.cloned.1.call-done = f32[64,2048]{1,0:T(8,128)} async-done(((f32[2048,2048]{1,0:T(8,128)}), f32[64,2048]{1,0:T(8,128)}) %reduce-scatter.9.cloned.1.call-update) | async-done | bytes 524304 | tf_op jit(solution)/shard_map/reduce_scatter | solution.py:34
  1351.9 187.4 %reduce-scatter.11.cloned.1.call-done = f32[64,2048]{1,0:T(8,128)} async-done(((f32[2048,2048]{1,0:T(8,128)}), f32[64,2048]{1,0:T(8,128)}) %reduce-scatter.11.cloned.1.call-update) | async-done | bytes 524304 | tf_op jit(solution)/shard_map/reduce_scatter | solution.py:35
  (30 shorter events, 0.1 us)
Async XLA Ops:
  7.2 605.6 %copy-start = (bf16[1,256,2048]{2,1,0:T(8,128)(2,1)S(1)}, bf16[1,256,2048]{2,1,0:T(8,128)(2,1)}, u32[]{:S(2)}) copy-start(bf16[1,256,2048]{2,1,0:T(8,128)(2,1)} %param.17) | copy-start | bytes 3145732
  7.2 3.8 copy-start.7
  7.2 191.8 %all-gather.6.cloned.1.call-start = ((), (), s32[]{:S(2)}) async-start(), calls=%async_computation.5 | async-start | bytes 8650752 | tf_op jit(solution)/shard_map/all_gather | solution.py:26
  9.1 197.2 %all-gather.8.cloned.1.call-start = ((), (), s32[]{:S(2)}) async-start(), calls=%async_computation.6 | async-start | bytes 8650752 | tf_op jit(solution)/shard_map/all_gather | solution.py:27
  11.0 521.7 %reduce-scatter.5.cloned.1.call-start = ((), (), s32[]{:S(2)}) async-start(), calls=%async_computation.4 | async-start | bytes 34603008 | tf_op jit(solution)/shard_map/reduce_scatter | solution.py:24
  128.1 1.0 copy-start.5
  128.1 1.9 copy-start.8
  128.1 70.9 %copy-start.2 = (bf16[1,256,2048]{2,1,0:T(8,128)(2,1)S(1)}, bf16[1,256,2048]{2,1,0:T(8,128)(2,1)}, u32[]{:S(2)}) copy-start(bf16[1,256,2048]{2,1,0:T(8,128)(2,1)} %param.15) | copy-start | bytes 3145732
  128.2 484.6 %all-gather.10.cloned.1.call-start = ((), (), s32[]{:S(2)}) async-start(), calls=%async_computation.7 | async-start | bytes 8650752 | tf_op jit(solution)/shard_map/all_gather | solution.py:28
  129.9 845.2 %all-gather.12.cloned.1.call-start = ((), (), s32[]{:S(2)}) async-start(), calls=%async_computation.8 | async-start | bytes 69206016 | tf_op jit(solution)/shard_map/all_gather | solution.py:42
  199.0 7.3 copy-start.3
  534.2 85.7 %copy-start.1 = (bf16[1,256,2048]{2,1,0:T(8,128)(2,1)S(1)}, bf16[1,256,2048]{2,1,0:T(8,128)(2,1)}, u32[]{:S(2)}) copy-start(bf16[1,256,2048]{2,1,0:T(8,128)(2,1)} %reduce-scatter.5.cloned.1.call-done) | copy-start | bytes 3145732
  621.7 542.8 %reduce-scatter.7.cloned.1.call-start = ((), (), s32[]{:S(2)}) async-start(), calls=%async_computation.9 | async-start | bytes 17301504 | tf_op jit(solution)/shard_map/reduce_scatter | solution.py:33
  630.3 1.2 copy-start.4
  630.3 721.6 %reduce-scatter.9.cloned.1.call-start = ((), (), s32[]{:S(2)}) async-start(), calls=%async_computation.10 | async-start | bytes 17301504 | tf_op jit(solution)/shard_map/reduce_scatter | solution.py:34
  639.9 899.5 %reduce-scatter.11.cloned.1.call-start = ((), (), s32[]{:S(2)}) async-start(), calls=%async_computation.11 | async-start | bytes 17301504 | tf_op jit(solution)/shard_map/reduce_scatter | solution.py:35
  648.1 0.8 copy-start.6
  691.5 13.8 slice-start
  698.4 6.9 slice-start.1
Sparse Core Ops, SparseCore 0:
  11.4 77.3 all-gather.5
  92.3 77.2 all-gather.7
  171.8 360.7 reduce-scatter.4
  535.9 76.7 all-gather.9
  621.8 353.1 all-gather.11
  977.8 186.6 reduce-scatter.6
  1167.4 184.5 reduce-scatter.8
  1354.8 184.5 reduce-scatter.10
where the time goes:
time: 1550 us
  waiting for transfers between devices  1120 us (72%)
  blocking collectives  140 us (9%)
  other arithmetic  137 us (9%)
  local copies, waits for them, and re-layouts  68.4 us (4%)
  matrix products  64.1 us (4%)
    reduce_scatter x1, waiting for transfers between devices, local_step(): lax.psum_scatter(part_rows, AXIS_NAME, scatter_dimension=0, tiled=True)  319 us
    all_gather x1, waiting for transfers between devices, local_step(): all_dx = lax.all_gather(d_x, AXIS_NAME, axis=0, tiled=True)  266 us
    reduce_scatter x1, waiting for transfers between devices, local_step(): lax.psum_scatter(jnp.einsum('bsd,bsf->df', normed, d_value, preferred_ele...  187 us
    reduce_scatter x1, waiting for transfers between devices, local_step(): lax.psum_scatter(jnp.einsum('bsd,bsf->df', normed, d_key, preferred_eleme...  187 us
    unnamed x2, blocking collectives  111 us
    scatter-add x1, other arithmetic, local_step(): jnp.zeros(embed_shard.shape, jnp.float32).at[scatter_ids]  106 us
    reduce_scatter x1, waiting for transfers between devices, local_step(): lax.psum_scatter(jnp.einsum('bsd,bsf->df', normed, d_query, preferred_ele...  83.5 us
    all_gather x1, waiting for transfers between devices, local_step(): lax.all_gather(wv_shard.astype(jnp.bfloat16), AXIS_NAME, axis=0, tiled=True)  78.6 us
  transfers between devices with their start and end apart: 8, of which 6 were waited for; matrix products, arithmetic and copies ran while one was open for 17% of the time, Pallas kernels for 0%

commit v1 on v0

v1 whole, which is shorter than its diff:
```python
import functools, heapq
import jax
import jax.numpy as jnp
from jax import lax
from jax.experimental import pallas as pl
from jax.experimental.pallas import tpu as pltpu
from jax.sharding import PartitionSpec as P

AXIS_NAME = "fsdp"
NUM_DEV = 32
DIM_SIZE = {"z": 4, "y": 2, "x": 2}


def coords():
    me = lax.axis_index(AXIS_NAME)
    return me // 8, (me // 4) % 2, (me // 2) % 2, me % 2


def dev_at(z, y, x, c):
    return ((z * 2 + y) * 2 + x) * 2 + c


def neighbour(dim):
    z, y, x, c = coords()
    if dim == "z":
        return dev_at((z + 1) % 4, y, x, c)
    if dim == "y":
        return dev_at(z, 1 - y, x, c)
    if dim == "x":
        return dev_at(z, y, 1 - x, c)
    return dev_at(z, y, x, 1 - c)


def entry_barrier():
    me = lax.axis_index(AXIS_NAME)
    barrier = pltpu.get_barrier_semaphore()

    def signal(step, carry):
        pl.semaphore_signal(barrier, inc=1, device_id=((me + step) % NUM_DEV,), device_id_type=pl.DeviceIdType.MESH)
        return carry

    lax.fori_loop(1, NUM_DEV, signal, 0)
    pl.semaphore_wait(barrier, NUM_DEV - 1)


def remote(src, dst, send_sem, recv_sem, dev):
    return pltpu.make_async_remote_copy(src_ref=src, dst_ref=dst, send_sem=send_sem, recv_sem=recv_sem,
                                        device_id=(dev,), device_id_type=pl.DeviceIdType.MESH)


def hop_plan(parts, reduce):
    free = {"z": 0.0, "y": 0.0, "x": 0.0}
    hops = []
    for size, order in parts:
        seq, held = [], 1.0 if not reduce else 16.0
        for dim in order:
            n = DIM_SIZE[dim]
            if reduce:
                held /= n
            seq += [(dim, held * size)] * (n - 1)
            if not reduce:
                held *= n
        hops.append(seq)
    heap, events = [], []

    def issue(part, k, now):
        dim, cost = hops[part][k]
        free[dim] = max(free[dim], now) + cost
        heapq.heappush(heap, (free[dim], part, k))

    for part in range(len(parts)):
        issue(part, 0, 0.0)
    while heap:
        now, part, k = heapq.heappop(heap)
        events.append((part, k))
        if k + 1 < len(hops[part]):
            issue(part, k + 1, now)
    return events


def gather_steps(order):
    steps, whole = [], []
    for dim in order:
        for ring in range(DIM_SIZE[dim] - 1):
            steps.append((dim, ring, tuple(whole)))
        whole.append(dim)
    return steps


def box(dim, ring, whole, shift):
    z, y, x, _ = coords()
    pos = {"z": z, "y": y, "x": x}
    idx = []
    for d in ("z", "y", "x"):
        if d == dim:
            at = (pos[d] + 2 * DIM_SIZE[d] - ring - shift) % DIM_SIZE[d]
            idx.append(pl.ds(at, 1))
        elif d in whole:
            idx.append(pl.ds(0, DIM_SIZE[d]))
        else:
            idx.append(pl.ds(pos[d], 1))
    return tuple(idx)


def gather_kernel(parts, n_arr, *refs):
    ins, outs = refs[:n_arr], refs[n_arr:2 * n_arr]
    ssem, rsem, csem, dsem, lsem = refs[2 * n_arr:]
    z, y, x, c = coords()
    here = (pl.ds(z, 1), pl.ds(y, 1), pl.ds(x, 1))
    entry_barrier()
    partner = neighbour("c")

    def cut(arr, idx, core, part):
        _, col, ncol, _ = part
        return outs[arr].at[idx[0], idx[1], idx[2], pl.ds(core, 1), :, pl.ds(col, ncol)]

    def own(part):
        return ins[part[0]].at[:, :, :, :, :, pl.ds(part[1], part[2])]

    steps = [gather_steps(p[3]) for p in parts]

    def hop(i, k):
        dim, ring, whole = steps[i][k]
        idx = box(dim, ring, whole, 0)
        src = own(parts[i]) if k == 0 else cut(parts[i][0], idx, c, parts[i])
        return remote(src, cut(parts[i][0], idx, c, parts[i]), ssem.at[i, k], rsem.at[i, k], neighbour(dim))

    def cross(i, k):
        if k < 0:
            idx, src = here, own(parts[i])
        else:
            idx = box(*steps[i][k], 1)
            src = cut(parts[i][0], idx, c, parts[i])
        return remote(src, cut(parts[i][0], idx, c, parts[i]), csem.at[i, k + 1], dsem.at[i, k + 1], partner)

    local = [pltpu.make_async_copy(own(p), cut(p[0], here, c, p), lsem.at[i]) for i, p in enumerate(parts)]
    for i in range(len(parts)):
        hop(i, 0).start()
    for i in range(len(parts)):
        local[i].start()
        cross(i, -1).start()
    for i in range(len(parts)):
        local[i].wait()
    for i, k in hop_plan([(p[2] * p[4], p[3]) for p in [(*q, 1.0) for q in parts]], False):
        hop(i, k).wait_recv()
        if k + 1 < len(steps[i]):
            hop(i, k + 1).start()
        cross(i, k).start()
    for i in range(len(parts)):
        for k in range(-1, len(steps[i])):
            cross(i, k).wait()
        for k in range(len(steps[i])):
            hop(i, k).wait_send()


def all_gather_blocks(arrays, parts, collective_id):
    n = len(arrays)
    blocks = [a.reshape(1, 1, 1, 1, *a.shape) for a in arrays]
    np_ = len(parts)
    outs = pl.pallas_call(
        functools.partial(gather_kernel, parts, n),
        out_shape=[jax.ShapeDtypeStruct((4, 2, 2, 2, *a.shape), a.dtype) for a in arrays],
        in_specs=[pl.BlockSpec(memory_space=pltpu.VMEM)] * n,
        out_specs=[pl.BlockSpec(memory_space=pl.ANY)] * n,
        scratch_shapes=[pltpu.SemaphoreType.DMA((np_, 5)), pltpu.SemaphoreType.DMA((np_, 5)),
                        pltpu.SemaphoreType.DMA((np_, 6)), pltpu.SemaphoreType.DMA((np_, 6)),
                        pltpu.SemaphoreType.DMA((np_,))],
        compiler_params=pltpu.CompilerParams(collective_id=collective_id, has_side_effects=True),
        name="gather_blocks",
    )(*blocks)
    return [o.reshape(NUM_DEV * a.shape[0], a.shape[1]) for o, a in zip(outs, arrays)]


def add_into(dst, src, rows):
    lead = dst.shape[:-2]
    count = 1
    for n in lead:
        count *= n
    step = 8
    per = rows // step

    def body(t, carry):
        blk, off = t // per, pl.multiple_of((t % per) * step, step)
        idx = []
        for n in reversed(lead):
            idx.append(blk % n)
            blk = blk // n
        at = (*reversed(idx), pl.ds(off, step), slice(None))
        dst[at] = dst[at] + src[at]
        return carry

    lax.fori_loop(0, count * per, body, 0)


def scatter_steps(order):
    steps, done = [], []
    for dim in order:
        for ring in range(DIM_SIZE[dim] - 1):
            steps.append((dim, ring, tuple(done)))
        done.append(dim)
    return steps


def left_shape(done):
    return tuple(1 if d in done else DIM_SIZE[d] for d in ("z", "y", "x"))


def reduce_kernel(parts, n_arr, rows, collect, *refs):
    ins, outs = refs[:n_arr], refs[n_arr:2 * n_arr]
    rest = refs[2 * n_arr:]
    n_part = len(parts)
    recv = []
    at = 0
    for p in parts:
        recv.append(rest[at:at + 5])
        at += 5
    own_buf = []
    for p in parts:
        n_own = DIM_SIZE[p[3][0]] - 1
        own_buf.append(rest[at:at + n_own])
        at += n_own
    ssem, rsem, lsem, osem, tsem, usem = rest[at:at + 6]
    gsem = rest[at + 6] if collect else None
    z, y, x, c = coords()
    me = lax.axis_index(AXIS_NAME)
    pos = {"z": z, "y": y, "x": x}
    steps = [scatter_steps(p[3]) for p in parts]

    def pick(ref, dim, index):
        sel = [pl.ds(index, 1) if d == dim else slice(None) for d in ("z", "y", "x")]
        return ref.at[sel[0], sel[1], sel[2]]

    def first(i, dim, index):
        arr, col, ncol, _ = parts[i]
        sel = [pl.ds(index, 1) if d == dim else slice(None) for d in ("z", "y", "x")]
        return ins[arr].at[sel[0], sel[1], sel[2], :, pl.ds(col, ncol)]

    def held(i, dim, index, k):
        return first(i, dim, index) if k == 0 else pick(recv[i][k - 1], dim, index)

    def keep_index(dim, ring):
        n = DIM_SIZE[dim]
        return (pos[dim] + 2 * n - ring - 2) % n if n > 2 else pos[dim]

    def hop(i, k):
        dim, ring, _ = steps[i][k]
        n = DIM_SIZE[dim]
        if ring == 0:
            src = held(i, dim, (pos[dim] + n - 1) % n, k)
        else:
            src = recv[i][k - 1]
        return remote(src, recv[i][k], ssem.at[i, k], rsem.at[i, k], neighbour(dim))

    def load(i, k):
        dim, ring, _ = steps[i][k]
        return pltpu.make_async_copy(first(i, dim, keep_index(dim, ring)), own_buf[i][k], lsem.at[i, k])

    entry_barrier()
    for i in range(n_part):
        hop(i, 0).start()
    for i in range(n_part):
        for k in range(len(own_buf[i])):
            load(i, k).start()

    def finish(i):
        arr, col, ncol, _ = parts[i]
        acc = recv[i][4]
        r = rows[arr]
        if arr in collect:
            idx = (pl.ds(z, 1), pl.ds(y, 1), pl.ds(x, 1), slice(None), pl.ds(c * collect[arr] + col, ncol))
            dst = outs[arr].at[idx]

            @pl.when(me != 0)
            def _():
                remote(acc, dst, tsem.at[i], gsem.at[i, me], 0).start()

            @pl.when(me == 0)
            def _():
                pltpu.make_async_copy(acc, dst, osem.at[i]).start()
            return
        half = r // 2
        cols = pl.ds(c * (outs[arr].shape[-1] // 2) + col, ncol)
        dst = outs[arr].at[:, :, :, :, cols]
        mine = acc.at[:, :, :, pl.ds(c * half, half), :]
        theirs = acc.at[:, :, :, pl.ds((1 - c) * half, half), :]
        remote(theirs, dst, tsem.at[i], usem.at[i], neighbour("c")).start()
        pltpu.make_async_copy(mine, dst, osem.at[i]).start()

    def finish_wait(i):
        arr, col, ncol, _ = parts[i]
        acc = recv[i][4]
        r = rows[arr]
        if arr in collect:
            dst = outs[arr].at[pl.ds(z, 1), pl.ds(y, 1), pl.ds(x, 1), :, pl.ds(c * collect[arr] + col, ncol)]

            @pl.when(me != 0)
            def _():
                remote(acc, dst, tsem.at[i], gsem.at[i, me], 0).wait_send()

            @pl.when(me == 0)
            def _():
                pltpu.make_async_copy(acc, dst, osem.at[i]).wait()

                def one(s, carry):
                    from_at = outs[arr].at[pl.ds(s // 8, 1), pl.ds((s // 4) % 2, 1), pl.ds((s // 2) % 2, 1), :,
                                           pl.ds(pl.multiple_of((s % 2) * collect[arr] + col, 128), ncol)]
                    remote(acc, from_at, tsem.at[i], gsem.at[i, s], 0).wait_recv()
                    return carry

                lax.fori_loop(1, NUM_DEV, one, 0)
            return
        half = r // 2
        cols = pl.ds(c * (outs[arr].shape[-1] // 2) + col, ncol)
        dst = outs[arr].at[:, :, :, :, cols]
        mine = acc.at[:, :, :, pl.ds(c * half, half), :]
        theirs = acc.at[:, :, :, pl.ds((1 - c) * half, half), :]
        remote(theirs, dst, tsem.at[i], usem.at[i], neighbour("c")).wait()
        pltpu.make_async_copy(mine, dst, osem.at[i]).wait()

    cost = [p[2] * rows[p[0]] for p in parts]
    for i, k in hop_plan(list(zip(cost, [p[3] for p in parts])), True):
        dim, ring, _ = steps[i][k]
        start = k - ring
        hop(i, k).wait_recv()
        if k < len(own_buf[i]):
            load(i, k).wait()
            src = own_buf[i][k]
        else:
            src = held(i, dim, keep_index(dim, ring), start)
        add_into(recv[i][k], src, rows[parts[i][0]])
        if k + 1 < 5:
            hop(i, k + 1).start()
        else:
            finish(i)
    for i in range(n_part):
        for k in range(5):
            hop(i, k).wait_send()
        finish_wait(i)


def reduce_scatter_blocks(arrays, parts, collect, collective_id):
    n = len(arrays)
    rows = [a.shape[0] // 16 for a in arrays]
    ins = [a.reshape(4, 2, 2, r, a.shape[1]) for a, r in zip(arrays, rows)]
    scratch = []
    for p in parts:
        for dim, ring, done in scatter_steps(p[3]):
            scratch.append(pltpu.VMEM((*left_shape(done + (dim,)), rows[p[0]], p[2]), jnp.float32))
    for p in parts:
        for k in range(DIM_SIZE[p[3][0]] - 1):
            scratch.append(pltpu.VMEM((*left_shape((p[3][0],)), rows[p[0]], p[2]), jnp.float32))
    m = len(parts)
    scratch += [pltpu.SemaphoreType.DMA((m, 5)), pltpu.SemaphoreType.DMA((m, 5)), pltpu.SemaphoreType.DMA((m, 3)),
                pltpu.SemaphoreType.DMA((m,)), pltpu.SemaphoreType.DMA((m,)), pltpu.SemaphoreType.DMA((m,))]
    out_shape = []
    for i, a in enumerate(arrays):
        if i in collect:
            out_shape.append(jax.ShapeDtypeStruct((4, 2, 2, rows[i], 2 * a.shape[1]), jnp.float32))
        else:
            out_shape.append(jax.ShapeDtypeStruct((1, 1, 1, rows[i] // 2, 2 * a.shape[1]), jnp.float32))
    if collect:
        scratch.append(pltpu.SemaphoreType.DMA((m, NUM_DEV)))
    outs = pl.pallas_call(
        functools.partial(reduce_kernel, parts, n, rows, {i: arrays[i].shape[1] for i in collect}),
        out_shape=out_shape,
        in_specs=[pl.BlockSpec(memory_space=pl.ANY)] * n,
        out_specs=[pl.BlockSpec(memory_space=pl.ANY)] * n,
        scratch_shapes=scratch,
        compiler_params=pltpu.CompilerParams(collective_id=collective_id, has_side_effects=True, vmem_limit_bytes=60 * 2**20),
        name="reduce_blocks",
    )(*ins)
    return [o.reshape(-1, o.shape[-1]) for o in outs]


def exchange_kernel(n_arr, has_hot, *refs):
    n_in = n_arr + has_hot
    srcs, dsts = refs[:n_arr], refs[n_in:n_in + n_arr]
    ssem, rsem, lsem = refs[2 * n_in:2 * n_in + 3]
    if has_hot:
        hot, hot_dst = refs[n_arr], refs[n_in + n_arr]
        hsem, gsem = refs[2 * n_in + 3:]
    me = lax.axis_index(AXIS_NAME)
    entry_barrier()

    def copy(a, step):
        to = (me + step) % NUM_DEV
        return remote(srcs[a].at[pl.ds(to, 1)], dsts[a].at[pl.ds(me, 1)], ssem.at[a, step], rsem.at[a, step], to)

    def local(a):
        return pltpu.make_async_copy(srcs[a].at[pl.ds(me, 1)], dsts[a].at[pl.ds(me, 1)], lsem.at[a])

    def hot_copy(to):
        return remote(hot.at[pl.ds(to, 1)], hot_dst, hsem.at[to], gsem, to)

    def start(step, carry):
        for a in range(n_arr):
            copy(a, step).start()
        return carry

    lax.fori_loop(1, NUM_DEV, start, 0)
    for a in range(n_arr):
        local(a).start()
    if has_hot:
        @pl.when(me == 0)
        def _():
            def hot_start(to, carry):
                hot_copy(to).start()
                return carry

            lax.fori_loop(1, NUM_DEV, hot_start, 0)
            mine = pltpu.make_async_copy(hot.at[pl.ds(0, 1)], hot_dst, lsem.at[n_arr])
            mine.start()
            mine.wait()

    def finish(step, carry):
        for a in range(n_arr):
            copy(a, step).wait()
        return carry

    lax.fori_loop(1, NUM_DEV, finish, 0)
    for a in range(n_arr):
        local(a).wait()
    if has_hot:
        @pl.when(me == 0)
        def _():
            def hot_end(to, carry):
                hot_copy(to).wait_send()
                return carry

            lax.fori_loop(1, NUM_DEV, hot_end, 0)

        @pl.when(me != 0)
        def _():
            hot_copy(0).wait_recv()


def exchange(blocks, hot, collective_id):
    any_spec = pl.BlockSpec(memory_space=pl.ANY)
    n = len(blocks)
    sems = [pltpu.SemaphoreType.DMA((n, NUM_DEV)), pltpu.SemaphoreType.DMA((n, NUM_DEV)), pltpu.SemaphoreType.DMA((n + 1,))]
    out_shape = [jax.ShapeDtypeStruct(b.shape, b.dtype) for b in blocks]
    args = list(blocks)
    if hot is not None:
        out_shape.append(jax.ShapeDtypeStruct((1, *hot.shape[1:]), hot.dtype))
        sems += [pltpu.SemaphoreType.DMA((NUM_DEV,)), pltpu.SemaphoreType.DMA]
        args.append(hot)
    return pl.pallas_call(
        functools.partial(exchange_kernel, n, int(hot is not None)),
        out_shape=out_shape,
        in_specs=[any_spec] * len(args),
        out_specs=[any_spec] * len(args),
        scratch_shapes=sems,
        compiler_params=pltpu.CompilerParams(collective_id=collective_id, has_side_effects=True),
        name="exchange",
    )(*args)


BLOCK = 8
MOST = 4
WIDE_OWNERS = ((1, 4, 4), (4, 9, 2))


def owner_blocks(owner):
    blocks = jnp.ones_like(owner)
    for first, last, n in WIDE_OWNERS:
        blocks = jnp.where((owner >= first) & (owner < last), n, blocks)
    return blocks


def cold_kernel(to_owner, src, dst, ssem, rsem):
    me = lax.axis_index(AXIS_NAME)
    entry_barrier()

    def copy(step, n):
        to = (me + step) % NUM_DEV
        return remote(src.at[pl.ds(to, 1), pl.ds(0, n)], dst.at[pl.ds(me, 1), pl.ds(0, n)], ssem.at[step], rsem.at[step], to)

    def by_size(owner, do):
        wide = owner < 0
        for first, last, n in WIDE_OWNERS:
            hit = (owner >= first) & (owner < last)
            wide = wide | hit
            pl.when(hit)(functools.partial(do, n))
        pl.when(jnp.logical_not(wide))(functools.partial(do, 1))

    def start(step, carry):
        by_size((me + step) % NUM_DEV if to_owner else me, lambda n: copy(step, n).start())
        return carry

    def finish(step, carry):
        by_size((me + step) % NUM_DEV if to_owner else me, lambda n: copy(step, n).wait_send())
        by_size(me if to_owner else (me - step + NUM_DEV) % NUM_DEV, lambda n: copy(step, n).wait_recv())
        return carry

    lax.fori_loop(1, NUM_DEV, start, 0)
    lax.fori_loop(1, NUM_DEV, finish, 0)


def cold_exchange(blocks, to_owner, collective_id):
    any_spec = pl.BlockSpec(memory_space=pl.ANY)
    return pl.pallas_call(
        functools.partial(cold_kernel, to_owner),
        out_shape=jax.ShapeDtypeStruct(blocks.shape, blocks.dtype),
        in_specs=[any_spec], out_specs=any_spec,
        scratch_shapes=[pltpu.SemaphoreType.DMA((NUM_DEV,)), pltpu.SemaphoreType.DMA((NUM_DEV,))],
        compiler_params=pltpu.CompilerParams(collective_id=collective_id, has_side_effects=True),
        name="cold_to_owner" if to_owner else "cold_to_device",
    )(blocks)


CAP = BLOCK * MOST


def add_kernel(ids, first, count, base, acc, rows, out, buf, sem, asem):
    def get(d, g):
        return pltpu.make_async_copy(rows.at[d, g], buf.at[d, g], sem.at[d, g])

    def each(do):
        def device(d, carry):
            def group(g, inner):
                do(d, g)
                return inner

            return lax.fori_loop(0, (count[d] + BLOCK - 1) // BLOCK, group, carry)

        lax.fori_loop(0, NUM_DEV, device, 0)

    each(lambda d, g: get(d, g).start())
    copy = pltpu.make_async_copy(acc, out, asem.at[0])
    copy.start()
    copy.wait()

    def add(d, g):
        get(d, g).wait()

        def row(r, carry):
            at = jnp.clip(ids[d, first[d] + BLOCK * g + r] - base[0], 0, out.shape[0] - 1)
            out[pl.ds(at, 1), :] += buf[d, g, pl.ds(r, 1), :]
            return carry

        lax.fori_loop(0, jnp.minimum(count[d] - BLOCK * g, BLOCK), row, 0)

    each(add)


def add_rows(ids, first, count, base, acc, rows):
    any_spec = pl.BlockSpec(memory_space=pl.ANY)
    return pl.pallas_call(
        add_kernel,
        out_shape=jax.ShapeDtypeStruct(acc.shape, jnp.float32),
        grid_spec=pltpu.PrefetchScalarGridSpec(
            num_scalar_prefetch=4, grid=(1,),
            in_specs=[any_spec, any_spec],
            out_specs=pl.BlockSpec(acc.shape, lambda i, *_: (0, 0)),
            scratch_shapes=[pltpu.VMEM((NUM_DEV, MOST, BLOCK, acc.shape[1]), jnp.float32),
                            pltpu.SemaphoreType.DMA((NUM_DEV, MOST)), pltpu.SemaphoreType.DMA((1,))]),
        compiler_params=pltpu.CompilerParams(vmem_limit_bytes=40 * 2**20),
        name="add_rows",
    )(ids, first, count, base, acc, rows)


GATHER_PARTS = [(0, 0, 1024, "xyz"), (0, 1024, 1024, "zyx"), (1, 0, 1024, "zxy"), (1, 1024, 1024, "zyx"),
                (2, 0, 1024, "zxy"), (2, 1024, 1024, "yxz"), (3, 0, 2048, "zxy")]
REDUCE_PARTS = [(3, 0, 1024, "xyz"), (0, 0, 1024, "yxz"), (1, 0, 1024, "xyz"), (2, 0, 512, "zxy"), (2, 512, 512, "yxz")]
HOT_ROWS = 1024


def norm_forward(x_rows, gain_full):
    inv_rms = lax.rsqrt(jnp.mean(x_rows * x_rows, axis=-1, keepdims=True) + 1e-5)
    h_rows = x_rows * inv_rms
    return inv_rms, h_rows, (h_rows * gain_full).astype(jnp.bfloat16)


def dot(a, b, dims, precision=None):
    return lax.dot_general(a, b, (dims, ((), ())), preferred_element_type=jnp.float32, precision=precision)


def solution(mesh):
    def local_step(tokens, embed_shard, gain_shard, wq_shard, wk_shard, wv_shard, d_query, d_key, d_value):
        vocab_local, width = embed_shard.shape
        n_tok = tokens.shape[1]
        me = lax.axis_index(AXIS_NAME)
        core = me % 2
        swap = [(d, d ^ 1) for d in range(NUM_DEV)]
        half = width // 2

        def partner(a):
            return lax.ppermute(a, AXIS_NAME, swap)

        def my_half(a, c):
            return lax.dynamic_slice_in_dim(a, c * half, half, axis=1)

        def paired(a):
            return jnp.concatenate([my_half(a, core), partner(my_half(a, 1 - core))], axis=0)

        tok = tokens[0]
        pos = jnp.arange(n_tok, dtype=jnp.int32)
        before = (tok[None, :] < tok[:, None]) | ((tok[None, :] == tok[:, None]) & (pos[None, :] < pos[:, None]))
        rank = jnp.sum(before.astype(jnp.int32), axis=1)
        place = rank[None, :] == pos[:, None]
        sorted_ids = jnp.sum(jnp.where(place, tok[None, :], 0), axis=1)

        hot_own = jnp.pad(embed_shard.astype(jnp.bfloat16), ((0, HOT_ROWS - vocab_local), (0, 0)))
        gain_rows = gain_shard.shape[0]
        ids_all, gains, hot_block = exchange(
            [jnp.broadcast_to(sorted_ids.reshape(1, 2, 128), (NUM_DEV, 2, 128)),
             jnp.broadcast_to(jnp.pad(gain_shard, (0, 128 - gain_rows)), (NUM_DEV, 1, 128))],
            hot_own.reshape(NUM_DEV, HOT_ROWS // NUM_DEV, width), 4)
        gain_full = gains[:, 0, :gain_rows].reshape(-1)
        ids_all = ids_all.reshape(NUM_DEV, n_tok)
        limits = vocab_local * jnp.arange(NUM_DEV + 1, dtype=jnp.int32)
        starts = jnp.sum((ids_all[:, :, None] < limits).astype(jnp.int32), axis=1)
        counts = (starts[:, 1:] - starts[:, :-1]).at[:, 0].set(0)
        owner_first = lax.dynamic_index_in_dim(starts, me, axis=1, keepdims=False)
        owner_count = lax.dynamic_index_in_dim(counts, me, axis=1, keepdims=False)
        my_first = lax.dynamic_index_in_dim(starts, me, axis=0, keepdims=False)[:NUM_DEV]
        my_count = lax.dynamic_index_in_dim(counts, me, axis=0, keepdims=False)
        base = (me * vocab_local).reshape(1)
        owners = jnp.arange(NUM_DEV, dtype=jnp.int32)
        slot = jnp.arange(CAP, dtype=jnp.int32)
        caps = BLOCK * owner_blocks(owners)
        my_cap = BLOCK * owner_blocks(me)
        rounds = jnp.maximum(jnp.max((counts + caps - 1) // caps), 1)
        tok_owner = tok // vocab_local
        tok_slot = rank - jnp.sum(jnp.where(tok_owner[:, None] == owners, my_first, 0), axis=1)
        tok_cap = BLOCK * owner_blocks(tok_owner)

        def cold_round(carry):
            step, cold = carry
            want = owner_first[:, None] + step * my_cap + slot
            ids = jnp.sum(jnp.where(want[:, :, None] == pos, ids_all[:, None, :], 0), axis=2) - base
            rows = jnp.take(embed_shard, jnp.clip(ids, 0, vocab_local - 1).reshape(-1), axis=0).astype(jnp.bfloat16)
            got = cold_exchange(rows.reshape(NUM_DEV, MOST, BLOCK, width), False, 6).reshape(-1, width)
            at = tok_slot - step * tok_cap
            here = (tok_owner > 0) & (at >= 0) & (at < tok_cap)
            mine = jnp.take(got, jnp.where(here, tok_owner * CAP + at, 0), axis=0)
            own = (tok_owner == me)[:, None]
            mine = jnp.where(own, jnp.take(rows, jnp.where(here, me * CAP + at, 0), axis=0), mine)
            return step + 1, jnp.where(here[:, None], mine, cold)

        _, cold = lax.while_loop(lambda carry: carry[0] < rounds, cold_round,
                                 (jnp.int32(0), jnp.zeros((n_tok, width), jnp.bfloat16)))

        shards = [w.astype(jnp.bfloat16) for w in (wq_shard, wk_shard, wv_shard)]
        wq_full, wk_full, wv_full, hot = all_gather_blocks([*shards, hot_block[0]], GATHER_PARTS, 1)

        hot_sel = ((tok[:, None] == jnp.arange(HOT_ROWS, dtype=jnp.int32)) & (tok[:, None] < vocab_local)).astype(jnp.bfloat16)
        x_rows = dot(hot_sel, hot, ((1,), (0,))) + cold.astype(jnp.float32)
        inv_rms, h_rows, normed = norm_forward(x_rows, gain_full)
        dq, dk, dv = d_query[0], d_key[0], d_value[0]
        normed_pair = jnp.concatenate([normed, partner(normed)], axis=0)
        d_w = [dot(normed_pair, paired(d), ((0,), (0,))) for d in (dq, dk, dv)]
        query_proj, key_proj, value_proj = [dot(normed, w, ((1,), (0,))).astype(jnp.bfloat16)[None]
                                            for w in (wq_full, wk_full, wv_full)]
        d_normed = (dot(dq, wq_full, ((1,), (1,))) + dot(dk, wk_full, ((1,), (1,))) + dot(dv, wv_full, ((1,), (1,))))
        gain_part = jnp.sum(d_normed * h_rows, axis=0)
        u_rows = d_normed * gain_full
        d_x = inv_rms * (u_rows - h_rows * jnp.mean(u_rows * h_rows, axis=-1, keepdims=True))

        pair_ids = jnp.concatenate([tok, partner(tok)])
        pair_sel = ((pair_ids[:, None] == jnp.arange(HOT_ROWS, dtype=jnp.int32)) & (pair_ids[:, None] < vocab_local)).astype(jnp.float32)
        hot_part = dot(pair_sel, paired(d_x), ((0,), (0,)), lax.Precision.HIGHEST)
        d_w_query, d_w_key, d_w_value, hot_sum = reduce_scatter_blocks([*d_w, hot_part], REDUCE_PARTS, (3,), 2)

        gain_blocks = jnp.pad(gain_part.reshape(NUM_DEV, 1, -1), ((0, 0), (0, 0), (0, 128 - gain_rows)))
        d_norm_gain = jnp.sum(exchange([gain_blocks], None, 5)[0], axis=(0, 1))[:gain_rows]
        d_embed = jnp.where(me == 0, hot_sum[:vocab_local], 0.0)

        def add_round(carry):
            step, total = carry
            want = my_first[:, None] + step * caps[:, None] + slot
            src = jnp.sum(jnp.where(want[:, :, None] == rank, pos, 0), axis=2)
            rows = jnp.take(d_x, src.reshape(-1), axis=0).reshape(NUM_DEV, MOST, BLOCK, width)
            got = cold_exchange(rows, True, 7)
            got = lax.dynamic_update_slice_in_dim(got, lax.dynamic_slice_in_dim(rows, me, 1, axis=0), me, axis=0)
            left = jnp.clip(owner_count - step * my_cap, 0, my_cap)
            return step + 1, add_rows(ids_all, owner_first + step * my_cap, left, base, total, got)

        _, d_embed = lax.while_loop(lambda carry: carry[0] < rounds, add_round, (jnp.int32(0), d_embed))
        return (query_proj, key_proj, value_proj, d_embed, d_norm_gain, d_w_query, d_w_key, d_w_value)

    row_spec = P(AXIS_NAME, None)
    act_spec = P(AXIS_NAME, None, None)
    vec_spec = P(AXIS_NAME)
    return jax.shard_map(local_step, mesh=mesh,
                         in_specs=(row_spec, row_spec, vec_spec, row_spec, row_spec, row_spec, act_spec, act_spec, act_spec),
                         out_specs=(act_spec, act_spec, act_spec, row_spec, vec_spec, row_spec, row_spec, row_spec),
                         check_vma=False)
```

time: 1550 us -> 896 us (0.58)
  waiting for transfers between devices: 1120 us -> 0.02 us
  Pallas kernels: 0 us -> 733 us
  blocking collectives: 140 us -> 0 us
  other arithmetic: 137 us -> 40.9 us
    reduce_scatter x4 -> x0, waiting for transfers between devices: 777 us -> none  [the longest x1 319 us: local_step(): lax.psum_scatter(part_rows, AXIS_NAME, scatter_dimension=0, tiled=True)]
    pallas_call x0 -> x7, Pallas kernels: none -> 733 us  [the longest x1 293 us: reduce_scatter_blocks(): pl.pallas_call(functools.partial(reduce_kernel, parts, n, rows, {i: array...]
    all_gather x4 -> x0, waiting for transfers between devices: 345 us -> none  [the longest x1 266 us: local_step(): all_dx = lax.all_gather(d_x, AXIS_NAME, axis=0, tiled=True)]
    unnamed x2 -> x0, blocking collectives: 111 us -> none
    scatter-add x1 -> x0, other arithmetic: 106 us -> none  [local_step(): jnp.zeros(embed_shard.shape, jnp.float32).at[scatter_ids]]
    gather x1 -> x4, local copies, waits for them, and re-layouts: 64.7 us -> 28.5 us  [the longest x1 11.5 us: cold_round(): jnp.take(embed_shard, jnp.clip(ids, 0, vocab_local - 1).reshape(-1), axis=0)]
    all_gather x1 -> x0, blocking collectives: 28.9 us -> none  [local_step(): all_tokens = lax.all_gather(tokens, AXIS_NAME, axis=0, tiled=True)]
    dot_general x9 -> x11, matrix products: 64.1 us -> 52.2 us  [dot(): lax.dot_general(a, b, (dims, ((), ())), preferred_element_type=jnp.float3...]
  transfers between devices with their start and end apart: 8 -> 6, of which waited for: 6 -> 0; matrix products, arithmetic and copies ran while one was open for 17% -> 12% of each run, Pallas kernels for 0% -> 32%
where the time goes in v1:
time: 896 us; the launch traced here: 892 us
  Pallas kernels  733 us (82%)
  local copies, waits for them, and re-layouts  62.4 us (7%)
  matrix products  52.2 us (6%)
  other arithmetic  40.9 us (5%)
    pallas_call x1, Pallas kernels, reduce_scatter_blocks(): pl.pallas_call(functools.partial(reduce_kernel, parts, n, rows, {i: array...  293 us
    pallas_call x1, Pallas kernels, all_gather_blocks(): pl.pallas_call(functools.partial(gather_kernel, parts, n), out_shape=[jax...  205 us
    pallas_call x2, Pallas kernels, cold_exchange(): pl.pallas_call(functools.partial(cold_kernel, to_owner), out_shape=jax.Sh...  199 us
    dot_general x11, matrix products, dot(): lax.dot_general(a, b, (dims, ((), ())), preferred_element_type=jnp.float3...  52.2 us
    pallas_call x2, Pallas kernels, exchange(): pl.pallas_call(functools.partial(exchange_kernel, n, int(hot is not None)...  26.8 us
  transfers between devices with their start and end apart: 6, of which 0 were waited for; matrix products, arithmetic and copies ran while one was open for 12% of the time, Pallas kernels for 32%

profile of v1, /device:TPU:14, one launch (start us, length us, event | category | flops | bytes accessed | tf_op | source)
XLA Modules:
  0.0 892.4 jit_solution(12291170493687362380)
XLA Ops:
  0.8 2.3 dynamic-slice_bitcast_fusion.5
  3.5 2.3 dynamic-slice_bitcast_fusion.3
  5.9 1.1 dynamic-slice_bitcast_fusion.1
  8.4 0.7 convert_bitcast_fusion.2.refs_0_
  9.1 4.0 convert.12
  13.1 1.9 copy-done.1
  15.0 2.5 pad.15
  18.8 19.5 %exchange.2 = (s32[32,2,128]{2,1,0:T(2,128)S(1)}, f32[32,1,128]{2,1,0:T(1,128)}, bf16[1,32,2048]{2,1,0:T(8,128)(2,1)}) custom-call(s32[32,2,128]{2,1,0:T(2,128)} %broadcast_in_dim.168.refs_0_, f32[32,1,128]{2,1,0:T(1,128)} %broadcast_in_dim.169.refs_1_, bf16[32,32,2048]{2,1,0:T(8,128)(2,1)} %bitcast.111), custom_call_target="tpu_custom_call" | custom-call | tf_op jit(solution)/shard_map/exchange/pallas_call | solution.py:447
  38.3 0.8 slice_reduce_fusion
  42.6 0.9 fusion.48
  44.8 90.2 %while.26 = (s32[]{:T(128)}, bf16[256,2048]{1,0:T(8,128)(2,1)S(1)}, s32[]{:T(128)}, s32[256]{0:T(256)S(1)}, s32[256]{0:T(256)S(1)}, /*index=5*/s32[256]{0:T(256)...) while((s32[]{:T(128)}, bf16[256,2048]{1,0:T(8,128)(2,1)S(1)}, ...), condition=%wide.region_8.10_spmd.clone, body=%wide.region_6.9_spmd.clone.sunk | while | flops 7104803 | bytes 33752620 | solution.py:641
  44.9 0.8 select_reduce_fusion.4
  46.1 11.5 %gather_fusion = bf16[1024,2048]{1,0:T(8,128)(2,1)} fusion(bf16[1000,2048]{1,0:T(8,128)(2,1)} %get-tuple-element.712, s32[1024]{0:T(1024)S(1)} %broadcast_clamp_fusion.4), kind=kCustom, calls=%fused_computation.3.clone.clone.1 | custom fusion | bytes 8392704 | tf_op jit(solution)/shard_map/while/body/jit(_take)/gather | solution.py:632
  57.6 4.9 select_convert_fusion.4.src
  62.6 56.8 %cold_to_device.2 = bf16[32,4,8,2048]{3,2,1,0:T(8,128)(2,1)} custom-call(bf16[32,4,8,2048]{3,2,1,0:T(8,128)(2,1)} %select_convert_fusion.4.src), custom_call_target="tpu_custom_call" | custom-call | tf_op jit(solution)/shard_map/while/body/cold_to_device/pallas_call | solution.py:501
  119.4 5.1 gather_fusion.1
  124.5 5.0 select_convert_fusion.5
  129.5 5.1 gather_fusion.2
  134.9 2.1 convert_bitcast_fusion
  137.0 205.2 %gather_blocks.1 = (bf16[4,2,2,2,64,2048]{5,4,3,2,1,0:T(8,128)(2,1)}, bf16[4,2,2,2,64,2048]{5,4,3,2,1,0:T(8,128)(2,1)}, bf16[4,2,2,2,64,2048]{5,4,3,2,1,0:T(8,128)(2,1)}, bf16[4,2,2,2,32,2048]{5,4,3,2,1,0:T(8,128)(2,1)}) custom-call(bf16[1,1,1,1,64,2048]{5,4,3,2,1,0:T(8,128)(2,1)} %convert_bitcast_fusion.2.refs_0_, ...), custom_call_target="tpu_custom_call" | custom-call | tf_op jit(solution)/shard_map/gather_blocks/pallas_call | solution.py:160
  342.2 3.8 multiply_reduce_fusion.2
  346.0 6.0 fusion.38
  352.1 2.4 convolution_add_fusion.1
  354.6 2.9 multiply_reduce_fusion
  358.4 3.3 fusion.17
  361.7 3.5 fusion.16
  365.3 3.4 fusion.15
  368.7 1.5 constant_dynamic-slice_fusion.2
  370.8 7.3 exchange.3
  378.2 1.3 reduce_sum.100
  380.8 7.2 fusion.28
  388.0 7.0 fusion.32
  395.1 7.1 fusion.24
  402.1 5.6 fusion.18
  407.8 293.5 %reduce_blocks.1 = (f32[1,1,1,64,2048]{4,3,2,1,0:T(8,128)}, f32[1,1,1,64,2048]{4,3,2,1,0:T(8,128)}, f32[1,1,1,64,2048]{4,3,2,1,0:T(8,128)}, f32[4,2,2,64,2048]{4,3,2,1,0:T(8,128)}) custom-call(f32[4,2,2,128,1024]{4,3,2,1,0:T(8,128)} %bitcast.114, f32[4,2,2,128,1024]{4,3,2,1,0:T(8,128)} %bitcast.112, f32[4,2,2,128,1024]{4,3,2,1,0:T(8,128)} %bitcast.113, ...), custom_call_target="tpu_custom_call" | custom-call | tf_op jit(solution)/shard_map/reduce_blocks/pallas_call | solution.py:363
  701.3 8.2 slice_select_fusion
  709.6 179.1 %while.27 = (s32[]{:T(128)}, f32[1000,2048]{1,0:T(8,128)}, s32[]{:T(128)}, s32[]{:T(128)}, s32[32]{0:T(128)S(1)}, /*index=5*/s32[32]{0:T(128)S(1)}, s32[32]{0:T(...) while((s32[]{:T(128)}, f32[1000,2048]{1,0:T(8,128)}, ...), condition=%wide.region_13.15_spmd.clone, body=%wide.region_11.14_spmd.clone.sunk | while | flops 2894276 | bytes 83290704 | solution.py:679
  709.6 7.6 copy.64.acc
  717.3 0.8 fusion.75
  718.4 6.9 gather_fusion.3
  725.3 7.3 broadcast_select_fusion.3.src
  732.5 142.3 %cold_to_owner.3 = f32[32,4,8,2048]{3,2,1,0:T(8,128)} custom-call(f32[32,4,8,2048]{3,2,1,0:T(8,128)} %broadcast_select_fusion.3.src), custom_call_target="tpu_custom_call" | custom-call | tf_op jit(solution)/shard_map/while/body/cold_to_owner/pallas_call | solution.py:501
  874.9 1.7 dynamic-slice_dynamic-update-slice_fusion.2.rows
  876.5 3.3 copy-done
  879.9 8.8 add_rows.3
  888.7 1.9 copy.65
  890.6 0.8 copy.66
  891.4 0.8 copy.67
  (119 shorter events, 11.8 us)
Async XLA Ops:
  0.6 7.4 copy-start.16
  0.6 5.2 copy-start.7
  0.7 7.7 copy-start.9
  0.7 378.8 %collective-permute-start.4 = (s32[256]{0:T(256)}, s32[256]{0:T(256)}, u32[]{:S(2)}, u32[]{:S(2)}) collective-permute-start(s32[256]{0:T(256)} %bitcast.128), channel_id=1, source_target_pairs={{0,1},{1,0},{2,3},{3,2},{4,5},{5,4},{6,7},{7,6},{8,9},{9,8},{10,11... | collective-permute-start | bytes 3080 | tf_op jit(solution)/shard_map/ppermute | solution.py:588
  3.1 392.0 %collective-permute-start.1 = (bf16[256,1024]{1,0:T(8,128)(2,1)}, bf16[256,1024]{1,0:T(8,128)(2,1)}, u32[]{:S(2)}, u32[]{:S(2)}) collective-permute-start(bf16[256,1024]{1,0:T(8,128)(2,1)} %get-tuple-element.489), channel_id=1, source_target_pairs={{0,1},{1,0},{2,3},{3,2},{4,5},{5,4},{6,7},{7,6},{8,9},{9,8},{10,11... | collective-permute-start | bytes 1572872 | tf_op jit(solution)/shard_map/ppermute | solution.py:588
  5.7 375.1 %collective-permute-start.2 = (bf16[256,1024]{1,0:T(8,128)(2,1)}, bf16[256,1024]{1,0:T(8,128)(2,1)}, u32[]{:S(2)}, u32[]{:S(2)}) collective-permute-start(bf16[256,1024]{1,0:T(8,128)(2,1)} %get-tuple-element.487), channel_id=1, source_target_pairs={{0,1},{1,0},{2,3},{3,2},{4,5},{5,4},{6,7},{7,6},{8,9},{9,8},{10,11... | collective-permute-start | bytes 1572872 | tf_op jit(solution)/shard_map/ppermute | solution.py:588
  6.9 381.1 %collective-permute-start.3 = (bf16[256,1024]{1,0:T(8,128)(2,1)}, bf16[256,1024]{1,0:T(8,128)(2,1)}, u32[]{:S(2)}, u32[]{:S(2)}) collective-permute-start(bf16[256,1024]{1,0:T(8,128)(2,1)} %get-tuple-element.485), channel_id=1, source_target_pairs={{0,1},{1,0},{2,3},{3,2},{4,5},{5,4},{6,7},{7,6},{8,9},{9,8},{10,11... | collective-permute-start | bytes 1572872 | tf_op jit(solution)/shard_map/ppermute | solution.py:588
  8.2 33.1 %copy-start.14 = (s32[256]{0:T(256)}, s32[256]{0:T(256)S(1)}, u32[]{:S(2)}) copy-start(s32[256]{0:T(256)S(1)} %convert_reduce_fusion.1) | copy-start | bytes 3076
  9.1 4.0 copy-start.20
  13.1 1.9 copy-start.1
  39.1 0.6 copy-start.2
  40.7 0.6 copy-start.17
  342.2 3.8 copy-start.5
  342.2 9.9 %slice-start.2 = ((s8[8388608]{0:T(1024)(128)(4,1)}), s8[4194304]{0:T(1024)(128)(4,1)S(1)}, s32[]{:S(2)}) async-start(s8[8388608]{0:T(1024)(128)(4,1)} %bitcast.142), calls=%async_computation.2 | async-start | bytes 8388608
  346.0 6.1 copy-start.6
  346.0 6.1 slice-start.3
  346.0 8.5 slice-start.4
  352.1 2.4 copy-start.8
  352.1 2.5 slice-start.5
  358.1 22.7 %collective-permute-start = (bf16[256,2048]{1,0:T(8,128)(2,1)S(1)}, bf16[256,2048]{1,0:T(8,128)(2,1)}, u32[]{:S(2)}, u32[]{:S(2)}) collective-permute-start(bf16[256,2048]{1,0:T(8,128)(2,1)S(1)} %get-tuple-element.481), channel_id=1, source_target_pairs={{0,1},{1,0},{2,3},{3,2},{4,5},{5,4},{6,7},{7,6},{8,9},{9,8},{10,11... | collective-permute-start | bytes 3145736 | tf_op jit(solution)/shard_map/ppermute | solution.py:588
  358.4 6.8 slice-start
  361.7 3.5 slice-start.1
  379.4 22.7 %collective-permute-start.5 = (f32[256,1024]{1,0:T(8,128)}, f32[256,1024]{1,0:T(8,128)S(1)}, u32[]{:S(2)}, u32[]{:S(2)}) collective-permute-start(f32[256,1024]{1,0:T(8,128)} %get-tuple-element.483), channel_id=1, source_target_pairs={{0,1},{1,0},{2,3},{3,2},{4,5},{5,4},{6,7},{7,6},{8,9},{9,8},{10,11... | collective-permute-start | bytes 3145736 | tf_op jit(solution)/shard_map/ppermute | solution.py:588
  380.8 7.2 copy-start.13
  388.0 7.0 copy-start.12
  395.1 7.1 copy-start.4
  701.3 8.3 copy-start.3
  701.3 8.3 copy-start.15
  701.3 8.3 copy-start.18
  701.3 8.2 copy-start.19
  709.5 181.0 %copy-start.11 = (f32[1,1,1,64,2048]{4,3,2,1,0:T(8,128)S(1)}, f32[1,1,1,64,2048]{4,3,2,1,0:T(8,128)}, u32[]{:S(2)}) copy-start(f32[1,1,1,64,2048]{4,3,2,1,0:T(8,128)} %get-tuple-element.351) | copy-start | bytes 1572868
  709.6 181.8 %copy-start.10 = (f32[1,1,1,64,2048]{4,3,2,1,0:T(8,128)S(1)}, f32[1,1,1,64,2048]{4,3,2,1,0:T(8,128)}, u32[]{:S(2)}) copy-start(f32[1,1,1,64,2048]{4,3,2,1,0:T(8,128)} %get-tuple-element.352) | copy-start | bytes 1572868
  876.5 3.3 copy-start

commit v2 on v1

--- a/solution.py
+++ b/solution.py
@@ -1,4 +1,4 @@
-import functools, heapq
+import functools
 import jax
 import jax.numpy as jnp
 from jax import lax
@@ -46,36 +46,6 @@
 def remote(src, dst, send_sem, recv_sem, dev):
     return pltpu.make_async_remote_copy(src_ref=src, dst_ref=dst, send_sem=send_sem, recv_sem=recv_sem,
                                         device_id=(dev,), device_id_type=pl.DeviceIdType.MESH)
-
-
-def hop_plan(parts, reduce):
-    free = {"z": 0.0, "y": 0.0, "x": 0.0}
-    hops = []
-    for size, order in parts:
-        seq, held = [], 1.0 if not reduce else 16.0
-        for dim in order:
-            n = DIM_SIZE[dim]
-            if reduce:
-                held /= n
-            seq += [(dim, held * size)] * (n - 1)
-            if not reduce:
-                held *= n
-        hops.append(seq)
-    heap, events = [], []
-
-    def issue(part, k, now):
-        dim, cost = hops[part][k]
-        free[dim] = max(free[dim], now) + cost
-        heapq.heappush(heap, (free[dim], part, k))
-
-    for part in range(len(parts)):
-        issue(part, 0, 0.0)
-    while heap:
-        now, part, k = heapq.heappop(heap)
-        events.append((part, k))
-        if k + 1 < len(hops[part]):
-            issue(part, k + 1, now)
-    return events
 
 
 def gather_steps(order):
@@ -102,10 +72,11 @@
     return tuple(idx)
 
 
-def gather_kernel(parts, n_arr, *refs):
+def gather_kernel(parts, first, events, n_arr, *refs):
     ins, outs = refs[:n_arr], refs[n_arr:2 * n_arr]
     ssem, rsem, csem, dsem, lsem = refs[2 * n_arr:]
     z, y, x, c = coords()
+    me = lax.axis_index(AXIS_NAME)
     here = (pl.ds(z, 1), pl.ds(y, 1), pl.ds(x, 1))
     entry_barrier()
     partner = neighbour("c")
@@ -133,15 +104,23 @@
             src = cut(parts[i][0], idx, c, parts[i])
         return remote(src, cut(parts[i][0], idx, c, parts[i]), csem.at[i, k + 1], dsem.at[i, k + 1], partner)
 
-    local = [pltpu.make_async_copy(own(p), cut(p[0], here, c, p), lsem.at[i]) for i, p in enumerate(parts)]
-    for i in range(len(parts)):
+    def local(i):
+        return pltpu.make_async_copy(own(parts[i]), cut(parts[i][0], here, c, parts[i]), lsem.at[i])
+
+    for i in first:
         hop(i, 0).start()
-    for i in range(len(parts)):
-        local[i].start()
+    for i in first:
+        local(i).start()
         cross(i, -1).start()
-    for i in range(len(parts)):
-        local[i].wait()
-    for i, k in hop_plan([(p[2] * p[4], p[3]) for p in [(*q, 1.0) for q in parts]], False):
+    for i in first:
+        local(i).wait()
+    for i, k in events:
+        if k < 0:
+            hop(i, 0).start()
+            local(i).start()
+            cross(i, -1).start()
+            local(i).wait()
+            continue
         hop(i, k).wait_recv()
         if k + 1 < len(steps[i]):
             hop(i, k + 1).start()
@@ -153,22 +132,20 @@
             hop(i, k).wait_send()
 
 
-def all_gather_blocks(arrays, parts, collective_id):
-    n = len(arrays)
-    blocks = [a.reshape(1, 1, 1, 1, *a.shape) for a in arrays]
-    np_ = len(parts)
+def all_gather_blocks(blocks, plan, collective_id):
+    parts, first, events = plan
+    n, m = len(blocks), len(parts)
     outs = pl.pallas_call(
-        functools.partial(gather_kernel, parts, n),
-        out_shape=[jax.ShapeDtypeStruct((4, 2, 2, 2, *a.shape), a.dtype) for a in arrays],
+        functools.partial(gather_kernel, parts, first, events, n),
+        out_shape=[jax.ShapeDtypeStruct((4, 2, 2, 2, *b.shape), b.dtype) for b in blocks],
         in_specs=[pl.BlockSpec(memory_space=pltpu.VMEM)] * n,
         out_specs=[pl.BlockSpec(memory_space=pl.ANY)] * n,
-        scratch_shapes=[pltpu.SemaphoreType.DMA((np_, 5)), pltpu.SemaphoreType.DMA((np_, 5)),
-                        pltpu.SemaphoreType.DMA((np_, 6)), pltpu.SemaphoreType.DMA((np_, 6)),
-                        pltpu.SemaphoreType.DMA((np_,))],
+        scratch_shapes=[pltpu.SemaphoreType.DMA((m, 5)), pltpu.SemaphoreType.DMA((m, 5)),
+                        pltpu.SemaphoreType.DMA((m, 6)), pltpu.SemaphoreType.DMA((m, 6)), pltpu.SemaphoreType.DMA((m,))],
         compiler_params=pltpu.CompilerParams(collective_id=collective_id, has_side_effects=True),
         name="gather_blocks",
-    )(*blocks)
-    return [o.reshape(NUM_DEV * a.shape[0], a.shape[1]) for o, a in zip(outs, arrays)]
+    )(*[b.reshape(1, 1, 1, 1, *b.shape) for b in blocks])
+    return [o.reshape(NUM_DEV * b.shape[0], b.shape[1]) for o, b in zip(outs, blocks)]
 
 
 def add_into(dst, src, rows):
@@ -205,7 +182,7 @@
     return tuple(1 if d in done else DIM_SIZE[d] for d in ("z", "y", "x"))
 
 
-def reduce_kernel(parts, n_arr, rows, collect, *refs):
+def reduce_kernel(parts, first_hops, events, n_arr, rows, collect, *refs):
     ins, outs = refs[:n_arr], refs[n_arr:2 * n_arr]
     rest = refs[2 * n_arr:]
     n_part = len(parts)
@@ -256,9 +233,9 @@
         return pltpu.make_async_copy(first(i, dim, keep_index(dim, ring)), own_buf[i][k], lsem.at[i, k])
 
     entry_barrier()
-    for i in range(n_part):
+    for i in first_hops:
         hop(i, 0).start()
-    for i in range(n_part):
+    for i in first_hops:
         for k in range(len(own_buf[i])):
             load(i, k).start()
 
@@ -317,8 +294,7 @@
         remote(theirs, dst, tsem.at[i], usem.at[i], neighbour("c")).wait()
         pltpu.make_async_copy(mine, dst, osem.at[i]).wait()
 
-    cost = [p[2] * rows[p[0]] for p in parts]
-    for i, k in hop_plan(list(zip(cost, [p[3] for p in parts])), True):
+    for i, k in events:
         dim, ring, _ = steps[i][k]
         start = k - ring
         hop(i, k).wait_recv()
@@ -338,7 +314,8 @@
         finish_wait(i)
 
 
-def reduce_scatter_blocks(arrays, parts, collect, collective_id):
+def reduce_scatter_blocks(arrays, plan, collect, collective_id):
+    parts, first, events = plan
     n = len(arrays)
     rows = [a.shape[0] // 16 for a in arrays]
     ins = [a.reshape(4, 2, 2, r, a.shape[1]) for a, r in zip(arrays, rows)]
@@ -361,7 +338,7 @@
     if collect:
         scratch.append(pltpu.SemaphoreType.DMA((m, NUM_DEV)))
     outs = pl.pallas_call(
-        functools.partial(reduce_kernel, parts, n, rows, {i: arrays[i].shape[1] for i in collect}),
+        functools.partial(reduce_kernel, parts, first, events, n, rows, {i: arrays[i].shape[1] for i in collect}),
         out_shape=out_shape,
         in_specs=[pl.BlockSpec(memory_space=pl.ANY)] * n,
         out_specs=[pl.BlockSpec(memory_space=pl.ANY)] * n,
@@ -372,13 +349,9 @@
     return [o.reshape(-1, o.shape[-1]) for o in outs]
 
 
-def exchange_kernel(n_arr, has_hot, *refs):
-    n_in = n_arr + has_hot
-    srcs, dsts = refs[:n_arr], refs[n_in:n_in + n_arr]
-    ssem, rsem, lsem = refs[2 * n_in:2 * n_in + 3]
-    if has_hot:
-        hot, hot_dst = refs[n_arr], refs[n_in + n_arr]
-        hsem, gsem = refs[2 * n_in + 3:]
+def exchange_kernel(n_arr, *refs):
+    srcs, dsts = refs[:n_arr], refs[n_arr:2 * n_arr]
+    ssem, rsem, lsem = refs[2 * n_arr:]
     me = lax.axis_index(AXIS_NAME)
     entry_barrier()
 
@@ -388,9 +361,6 @@
 
     def local(a):
         return pltpu.make_async_copy(srcs[a].at[pl.ds(me, 1)], dsts[a].at[pl.ds(me, 1)], lsem.at[a])
-
-    def hot_copy(to):
-        return remote(hot.at[pl.ds(to, 1)], hot_dst, hsem.at[to], gsem, to)
 
     def start(step, carry):
         for a in range(n_arr):
@@ -400,17 +370,6 @@
     lax.fori_loop(1, NUM_DEV, start, 0)
     for a in range(n_arr):
         local(a).start()
-    if has_hot:
-        @pl.when(me == 0)
-        def _():
-            def hot_start(to, carry):
-                hot_copy(to).start()
-                return carry
-
-            lax.fori_loop(1, NUM_DEV, hot_start, 0)
-            mine = pltpu.make_async_copy(hot.at[pl.ds(0, 1)], hot_dst, lsem.at[n_arr])
-            mine.start()
-            mine.wait()
 
     def finish(step, carry):
         for a in range(n_arr):
@@ -420,44 +379,25 @@
     lax.fori_loop(1, NUM_DEV, finish, 0)
     for a in range(n_arr):
         local(a).wait()
-    if has_hot:
-        @pl.when(me == 0)
-        def _():
-            def hot_end(to, carry):
-                hot_copy(to).wait_send()
-                return carry
-
-            lax.fori_loop(1, NUM_DEV, hot_end, 0)
-
-        @pl.when(me != 0)
-        def _():
-            hot_copy(0).wait_recv()
-
-
-def exchange(blocks, hot, collective_id):
-    any_spec = pl.BlockSpec(memory_space=pl.ANY)
+
+
+def exchange(blocks, collective_id):
     n = len(blocks)
-    sems = [pltpu.SemaphoreType.DMA((n, NUM_DEV)), pltpu.SemaphoreType.DMA((n, NUM_DEV)), pltpu.SemaphoreType.DMA((n + 1,))]
-    out_shape = [jax.ShapeDtypeStruct(b.shape, b.dtype) for b in blocks]
-    args = list(blocks)
-    if hot is not None:
-        out_shape.append(jax.ShapeDtypeStruct((1, *hot.shape[1:]), hot.dtype))
-        sems += [pltpu.SemaphoreType.DMA((NUM_DEV,)), pltpu.SemaphoreType.DMA]
-        args.append(hot)
+    specs = [pl.BlockSpec(memory_space=pl.ANY)] * n
     return pl.pallas_call(
-        functools.partial(exchange_kernel, n, int(hot is not None)),
-        out_shape=out_shape,
-        in_specs=[any_spec] * len(args),
-        out_specs=[any_spec] * len(args),
-        scratch_shapes=sems,
+        functools.partial(exchange_kernel, n),
+        out_shape=[jax.ShapeDtypeStruct(b.shape, b.dtype) for b in blocks],
+        in_specs=specs, out_specs=specs,
+        scratch_shapes=[pltpu.SemaphoreType.DMA((n, NUM_DEV)), pltpu.SemaphoreType.DMA((n, NUM_DEV)),
+                        pltpu.SemaphoreType.DMA((n,))],
         compiler_params=pltpu.CompilerParams(collective_id=collective_id, has_side_effects=True),
         name="exchange",
-    )(*args)
+    )(*blocks)
 
 
 BLOCK = 8
 MOST = 4
-WIDE_OWNERS = ((1, 4, 4), (4, 9, 2))
+WIDE_OWNERS = ((1, 2, 4), (2, 4, 3), (4, 9, 2))
 
 
 def owner_blocks(owner):
@@ -467,13 +407,20 @@
     return blocks
 
 
-def cold_kernel(to_owner, src, dst, ssem, rsem):
+def cold_kernel(to_owner, *refs):
+    if to_owner:
+        src, dst, ssem, rsem, lsem = refs
+    else:
+        src, rows, dst, row_dst, ssem, rsem, lsem, hsem, gsem = refs
     me = lax.axis_index(AXIS_NAME)
     entry_barrier()
 
     def copy(step, n):
         to = (me + step) % NUM_DEV
         return remote(src.at[pl.ds(to, 1), pl.ds(0, n)], dst.at[pl.ds(me, 1), pl.ds(0, n)], ssem.at[step], rsem.at[step], to)
+
+    def hand(to):
+        return remote(rows.at[pl.ds(to, 1)], row_dst, hsem.at[to], gsem.at[0], to)
 
     def by_size(owner, do):
         wide = owner < 0
@@ -492,26 +439,56 @@
         by_size(me if to_owner else (me - step + NUM_DEV) % NUM_DEV, lambda n: copy(step, n).wait_recv())
         return carry
 
+    def each(do):
+        def body(to, carry):
+            do(hand(to))
+            return carry
+
+        lax.fori_loop(1, NUM_DEV, body, 0)
+
+    local = pltpu.make_async_copy(src.at[pl.ds(me, 1)], dst.at[pl.ds(me, 1)], lsem)
     lax.fori_loop(1, NUM_DEV, start, 0)
+    local.start()
+    if not to_owner:
+        @pl.when(me == 0)
+        def _():
+            each(lambda c: c.start())
+            mine = pltpu.make_async_copy(rows.at[pl.ds(0, 1)], row_dst, gsem.at[1])
+            mine.start()
+            mine.wait()
+
     lax.fori_loop(1, NUM_DEV, finish, 0)
-
-
-def cold_exchange(blocks, to_owner, collective_id):
-    any_spec = pl.BlockSpec(memory_space=pl.ANY)
+    local.wait()
+    if not to_owner:
+        @pl.when(me == 0)
+        def _():
+            each(lambda c: c.wait_send())
+
+        @pl.when(me != 0)
+        def _():
+            hand(0).wait_recv()
+
+
+def cold_exchange(arrays, collective_id):
+    to_owner = len(arrays) == 1
+    specs = [pl.BlockSpec(memory_space=pl.ANY)] * len(arrays)
+    sems = [pltpu.SemaphoreType.DMA((NUM_DEV,)), pltpu.SemaphoreType.DMA((NUM_DEV,)), pltpu.SemaphoreType.DMA]
+    out_shape = [jax.ShapeDtypeStruct(arrays[0].shape, arrays[0].dtype)]
+    if not to_owner:
+        out_shape.append(jax.ShapeDtypeStruct((1, *arrays[1].shape[1:]), arrays[1].dtype))
+        sems += [pltpu.SemaphoreType.DMA((NUM_DEV,)), pltpu.SemaphoreType.DMA((2,))]
     return pl.pallas_call(
         functools.partial(cold_kernel, to_owner),
-        out_shape=jax.ShapeDtypeStruct(blocks.shape, blocks.dtype),
-        in_specs=[any_spec], out_specs=any_spec,
-        scratch_shapes=[pltpu.SemaphoreType.DMA((NUM_DEV,)), pltpu.SemaphoreType.DMA((NUM_DEV,))],
+        out_shape=out_shape, in_specs=specs, out_specs=specs, scratch_shapes=sems,
         compiler_params=pltpu.CompilerParams(collective_id=collective_id, has_side_effects=True),
         name="cold_to_owner" if to_owner else "cold_to_device",
-    )(blocks)
+    )(*arrays)
 
 
 CAP = BLOCK * MOST
 
 
-def add_kernel(ids, first, count, base, acc, rows, out, buf, sem, asem):
+def add_kernel(fresh, ids, first, count, base, acc, rows, out, buf, sem, asem):
     def get(d, g):
         return pltpu.make_async_copy(rows.at[d, g], buf.at[d, g], sem.at[d, g])
 
@@ -526,9 +503,23 @@
         lax.fori_loop(0, NUM_DEV, device, 0)
 
     each(lambda d, g: get(d, g).start())
-    copy = pltpu.make_async_copy(acc, out, asem.at[0])
-    copy.start()
-    copy.wait()
+    def fill():
+        copy = pltpu.make_async_copy(acc.at[pl.ds(0, out.shape[0])], out, asem.at[0])
+        copy.start()
+        copy.wait()
+
+    if fresh:
+        pl.when(base[0] == 0)(fill)
+
+        @pl.when(base[0] != 0)
+        def _():
+            def zero(t, carry):
+                out[pl.ds(pl.multiple_of(t * 8, 8), 8), :] = jnp.zeros((8, out.shape[1]), jnp.float32)
+                return carry
+
+            lax.fori_loop(0, out.shape[0] // 8, zero, 0)
+    else:
+        fill()
 
     def add(d, g):
         get(d, g).wait()
@@ -543,15 +534,15 @@
     each(add)
 
 
-def add_rows(ids, first, count, base, acc, rows):
+def add_rows(fresh, n_out, ids, first, count, base, acc, rows):
     any_spec = pl.BlockSpec(memory_space=pl.ANY)
     return pl.pallas_call(
-        add_kernel,
-        out_shape=jax.ShapeDtypeStruct(acc.shape, jnp.float32),
+        functools.partial(add_kernel, fresh),
+        out_shape=jax.ShapeDtypeStruct((n_out, acc.shape[1]), jnp.float32),
         grid_spec=pltpu.PrefetchScalarGridSpec(
             num_scalar_prefetch=4, grid=(1,),
             in_specs=[any_spec, any_spec],
-            out_specs=pl.BlockSpec(acc.shape, lambda i, *_: (0, 0)),
+            out_specs=pl.BlockSpec((n_out, acc.shape[1]), lambda i, *_: (0, 0)),
             scratch_shapes=[pltpu.VMEM((NUM_DEV, MOST, BLOCK, acc.shape[1]), jnp.float32),
                             pltpu.SemaphoreType.DMA((NUM_DEV, MOST)), pltpu.SemaphoreType.DMA((1,))]),
         compiler_params=pltpu.CompilerParams(vmem_limit_bytes=40 * 2**20),
@@ -559,9 +550,44 @@
     )(ids, first, count, base, acc, rows)
 
 
-GATHER_PARTS = [(0, 0, 1024, "xyz"), (0, 1024, 1024, "zyx"), (1, 0, 1024, "zxy"), (1, 1024, 1024, "zyx"),
-                (2, 0, 1024, "zxy"), (2, 1024, 1024, "yxz"), (3, 0, 2048, "zxy")]
-REDUCE_PARTS = [(3, 0, 1024, "xyz"), (0, 0, 1024, "yxz"), (1, 0, 1024, "xyz"), (2, 0, 512, "zxy"), (2, 512, 512, "yxz")]
+def make_plan(parts, started, awaited):
+    begin, cuts = {}, []
+    for arr, tiles, order in parts:
+        cuts.append((arr, begin.get(arr, 0), 128 * tiles, order))
+        begin[arr] = begin.get(arr, 0) + 128 * tiles
+    first = [ord(p) - ord("a") for p in started]
+    at = [0 if i in first else -1 for i in range(len(parts))]
+    events = []
+    for letter in awaited:
+        i = ord(letter) - ord("a")
+        events.append((i, at[i]))
+        at[i] += 1
+    return cuts, first, events
+
+
+GATHER_PLAN = make_plan(
+    ((0, 8, 'zxy'),
+     (0, 8, 'zyx'),
+     (1, 4, 'zxy'),
+     (1, 12, 'yzx'),
+     (2, 7, 'yxz'),
+     (2, 7, 'zxy'),
+     (2, 2, 'yxz'),
+     (3, 16, 'xzy')),
+    "adbcfeg", "ebfgcbcabfcafdecadhbfhdhcgadhghegefgbadeh")
+REDUCE_PLAN = make_plan(
+    ((3, 4, 'yxz'),
+     (3, 4, 'xyz'),
+     (0, 3, 'xzy'),
+     (0, 2, 'yxz'),
+     (0, 3, 'yxz'),
+     (1, 4, 'yxz'),
+     (1, 1, 'zxy'),
+     (1, 3, 'yxz'),
+     (2, 1, 'xzy'),
+     (2, 5, 'zyx'),
+     (2, 2, 'xyz')),
+    "adefhbigcjk", "gabjgdcijgecikadjgcfiadeciadeafdhefbefhbkfhbjkghcibjkhk")
 HOT_ROWS = 1024
 
 
@@ -602,10 +628,9 @@
 
         hot_own = jnp.pad(embed_shard.astype(jnp.bfloat16), ((0, HOT_ROWS - vocab_local), (0, 0)))
         gain_rows = gain_shard.shape[0]
-        ids_all, gains, hot_block = exchange(
+        ids_all, gains = exchange(
             [jnp.broadcast_to(sorted_ids.reshape(1, 2, 128), (NUM_DEV, 2, 128)),
-             jnp.broadcast_to(jnp.pad(gain_shard, (0, 128 - gain_rows)), (NUM_DEV, 1, 128))],
-            hot_own.reshape(NUM_DEV, HOT_ROWS // NUM_DEV, width), 4)
+             jnp.broadcast_to(jnp.pad(gain_shard, (0, 128 - gain_rows)), (NUM_DEV, 1, 128))], 4)
         gain_full = gains[:, 0, :gain_rows].reshape(-1)
         ids_all = ids_all.reshape(NUM_DEV, n_tok)
         limits = vocab_local * jnp.arange(NUM_DEV + 1, dtype=jnp.int32)
@@ -626,23 +651,23 @@
         tok_cap = BLOCK * owner_blocks(tok_owner)
 
         def cold_round(carry):
-            step, cold = carry
+            step, cold, _ = carry
             want = owner_first[:, None] + step * my_cap + slot
             ids = jnp.sum(jnp.where(want[:, :, None] == pos, ids_all[:, None, :], 0), axis=2) - base
-            rows = jnp.take(embed_shard, jnp.clip(ids, 0, vocab_local - 1).reshape(-1), axis=0).astype(jnp.bfloat16)
-            got = cold_exchange(rows.reshape(NUM_DEV, MOST, BLOCK, width), False, 6).reshape(-1, width)
+            pick = (ids.reshape(-1, 1) == jnp.arange(HOT_ROWS, dtype=jnp.int32)).astype(jnp.bfloat16)
+            rows = dot(pick, hot_own, ((1,), (0,))).astype(jnp.bfloat16)
+            got, handed = cold_exchange([rows.reshape(NUM_DEV, MOST, BLOCK, width), hot_blocks], 6)
             at = tok_slot - step * tok_cap
             here = (tok_owner > 0) & (at >= 0) & (at < tok_cap)
-            mine = jnp.take(got, jnp.where(here, tok_owner * CAP + at, 0), axis=0)
-            own = (tok_owner == me)[:, None]
-            mine = jnp.where(own, jnp.take(rows, jnp.where(here, me * CAP + at, 0), axis=0), mine)
-            return step + 1, jnp.where(here[:, None], mine, cold)
-
-        _, cold = lax.while_loop(lambda carry: carry[0] < rounds, cold_round,
-                                 (jnp.int32(0), jnp.zeros((n_tok, width), jnp.bfloat16)))
+            mine = jnp.take(got.reshape(-1, width), jnp.where(here, tok_owner * CAP + at, 0), axis=0)
+            return step + 1, jnp.where(here[:, None], mine, cold), handed
+
+        hot_blocks = hot_own.reshape(NUM_DEV, HOT_ROWS // NUM_DEV, width)
+        carry = cold_round((jnp.int32(0), jnp.zeros((n_tok, width), jnp.bfloat16), None))
+        _, cold, handed = lax.while_loop(lambda carry: carry[0] < rounds, cold_round, carry)
 
         shards = [w.astype(jnp.bfloat16) for w in (wq_shard, wk_shard, wv_shard)]
-        wq_full, wk_full, wv_full, hot = all_gather_blocks([*shards, hot_block[0]], GATHER_PARTS, 1)
+        wq_full, wk_full, wv_full, hot = all_gather_blocks([*shards, handed[0]], GATHER_PLAN, 1)
 
         hot_sel = ((tok[:, None] == jnp.arange(HOT_ROWS, dtype=jnp.int32)) & (tok[:, None] < vocab_local)).astype(jnp.bfloat16)
         x_rows = dot(hot_sel, hot, ((1,), (0,))) + cold.astype(jnp.float32)
@@ -660,23 +685,21 @@
         pair_ids = jnp.concatenate([tok, partner(tok)])
         pair_sel = ((pair_ids[:, None] == jnp.arange(HOT_ROWS, dtype=jnp.int32)) & (pair_ids[:, None] < vocab_local)).astype(jnp.float32)
         hot_part = dot(pair_sel, paired(d_x), ((0,), (0,)), lax.Precision.HIGHEST)
-        d_w_query, d_w_key, d_w_value, hot_sum = reduce_scatter_blocks([*d_w, hot_part], REDUCE_PARTS, (3,), 2)
+        d_w_query, d_w_key, d_w_value, hot_sum = reduce_scatter_blocks([*d_w, hot_part], REDUCE_PLAN, (3,), 2)
 
         gain_blocks = jnp.pad(gain_part.reshape(NUM_DEV, 1, -1), ((0, 0), (0, 0), (0, 128 - gain_rows)))
-        d_norm_gain = jnp.sum(exchange([gain_blocks], None, 5)[0], axis=(0, 1))[:gain_rows]
-        d_embed = jnp.where(me == 0, hot_sum[:vocab_local], 0.0)
-
-        def add_round(carry):
-            step, total = carry
+        d_norm_gain = jnp.sum(exchange([gain_blocks], 5)[0], axis=(0, 1))[:gain_rows]
+        def add_round(step, total, fresh):
             want = my_first[:, None] + step * caps[:, None] + slot
             src = jnp.sum(jnp.where(want[:, :, None] == rank, pos, 0), axis=2)
             rows = jnp.take(d_x, src.reshape(-1), axis=0).reshape(NUM_DEV, MOST, BLOCK, width)
-            got = cold_exchange(rows, True, 7)
-            got = lax.dynamic_update_slice_in_dim(got, lax.dynamic_slice_in_dim(rows, me, 1, axis=0), me, axis=0)
+            got = cold_exchange([rows], 7)[0]
             left = jnp.clip(owner_count - step * my_cap, 0, my_cap)
-            return step + 1, add_rows(ids_all, owner_first + step * my_cap, left, base, total, got)
-
-        _, d_embed = lax.while_loop(lambda carry: carry[0] < rounds, add_round, (jnp.int32(0), d_embed))
+            return add_rows(fresh, vocab_local, ids_all, owner_first + step * my_cap, left, base, total, got)
+
+        _, d_embed = lax.while_loop(lambda carry: carry[0] < rounds,
+                                    lambda carry: (carry[0] + 1, add_round(*carry, False)),
+                                    (jnp.int32(1), add_round(jnp.int32(0), hot_sum, True)))
         return (query_proj, key_proj, value_proj, d_embed, d_norm_gain, d_w_query, d_w_key, d_w_value)
 
     row_spec = P(AXIS_NAME, None)

time: 896 us -> 746 us (0.83)
  the two profiles are of different devices: /device:TPU:14 before, /device:TPU:1 now
where the time goes in v2:
time: 746 us; the launch traced here: 739 us
  Pallas kernels  615 us (82%)
  matrix products  62.6 us (8%)
  local copies, waits for them, and re-layouts  31.7 us (4%)
  other arithmetic  25.1 us (3%)
    pallas_call x1, Pallas kernels, reduce_scatter_blocks(): pl.pallas_call(functools.partial(reduce_kernel, parts, first, events, n,...  251 us
    pallas_call x1, Pallas kernels, all_gather_blocks(): pl.pallas_call(functools.partial(gather_kernel, parts, first, events, n),...  133 us
    pallas_call x2, Pallas kernels, cold_exchange(): pl.pallas_call(functools.partial(cold_kernel, to_owner), out_shape=out_sh...  129 us
    pallas_call x2, Pallas kernels, exchange(): pl.pallas_call(functools.partial(exchange_kernel, n), out_shape=[jax.Shap...  83.4 us
    dot_general x12, matrix products, dot(): lax.dot_general(a, b, (dims, ((), ())), preferred_element_type=jnp.float3...  62.6 us
    pallas_call x1, Pallas kernels, add_rows(): pl.pallas_call(functools.partial(add_kernel, fresh), out_shape=jax.ShapeD...  18.9 us
  transfers between devices with their start and end apart: 6, of which 0 were waited for; matrix products, arithmetic and copies ran while one was open for 14% of the time, Pallas kernels for 47%

profile of v2, /device:TPU:1, one launch (start us, length us, event | category | flops | bytes accessed | tf_op | source)
XLA Modules:
  0.0 739.0 jit_solution(11464718662745190452)
XLA Ops:
  0.7 2.2 dynamic-slice_bitcast_fusion.5
  3.4 0.9 convert_reduce_fusion.1
  4.4 0.7 and_select_fusion.14
  5.0 0.6 compare_reduce_fusion
  5.7 0.7 broadcast_compare_fusion.2
  6.4 0.8 select_reduce_fusion.3
  7.2 0.7 pad.14
  9.1 11.1 %exchange.2 = (s32[32,2,128]{2,1,0:T(2,128)S(1)}, f32[32,1,128]{2,1,0:T(1,128)}) custom-call(s32[32,2,128]{2,1,0:T(2,128)} %broadcast_in_dim.202.refs_0_, f32[32,1,128]{2,1,0:T(1,128)} %broadcast_in_dim.203.refs_1_), custom_call_target="tpu_custom_call" | custom-call | tf_op jit(solution)/shard_map/exchange/pallas_call | solution.py:387
  20.3 0.7 convert_reduce_fusion
  21.1 0.8 select_reduce_fusion.2
  22.0 4.0 convert_element_type.54
  25.9 6.2 fusion.17
  32.1 2.4 pad.15
  34.9 0.7 broadcast_select_fusion.2
  35.6 0.9 fusion.53
  37.1 75.5 %cold_to_device.2 = (bf16[32,4,8,2048]{3,2,1,0:T(8,128)(2,1)}, bf16[1,32,2048]{2,1,0:T(8,128)(2,1)}) custom-call(bf16[32,4,8,2048]{3,2,1,0:T(8,128)(2,1)} %bitcast.151, bf16[32,32,2048]{2,1,0:T(8,128)(2,1)} %bitcast.140), custom_call_target="tpu_custom_call" | custom-call | tf_op jit(solution)/shard_map/cold_to_device/pallas_call | solution.py:480
  112.6 5.1 gather_fusion.2
  118.1 1.9 convert_bitcast_fusion.2.refs_0_
  120.0 0.9 convert_bitcast_fusion
  120.9 132.7 %gather_blocks.1 = (bf16[4,2,2,2,64,2048]{5,4,3,2,1,0:T(8,128)(2,1)}, bf16[4,2,2,2,64,2048]{5,4,3,2,1,0:T(8,128)(2,1)}, bf16[4,2,2,2,64,2048]{5,4,3,2,1,0:T(8,128)(2,1)}, bf16[4,2,2,2,32,2048]{5,4,3,2,1,0:T(8,128)(2,1)}) custom-call(bf16[1,1,1,1,64,2048]{5,4,3,2,1,0:T(8,128)(2,1)} %convert_bitcast_fusion.2.refs_0_, ...), custom_call_target="tpu_custom_call" | custom-call | tf_op jit(solution)/shard_map/gather_blocks/pallas_call | solution.py:138
  253.6 4.9 multiply_reduce_fusion.2
  258.7 5.9 fusion.43
  264.8 2.4 convolution_add_fusion.1
  267.2 1.1 slice-done.1
  268.3 2.8 multiply_reduce_fusion
  272.0 1.1 dynamic-slice_bitcast_fusion.3
  273.4 1.1 dynamic-slice_bitcast_fusion.1
  274.7 3.3 fusion.19
  278.0 3.7 fusion.20
  281.8 0.8 select_reduce_fusion.1
  282.9 6.8 gather_fusion.3
  289.7 7.2 broadcast_select_fusion.1.refs_0_
  296.9 6.7 fusion.21
  303.6 1.5 constant_dynamic-slice_fusion.1
  305.1 53.8 %cold_to_owner.2.rows = f32[32,4,8,2048]{3,2,1,0:T(8,128)} custom-call(f32[32,4,8,2048]{3,2,1,0:T(8,128)} %broadcast_select_fusion.1.refs_0_), custom_call_target="tpu_custom_call" | custom-call | tf_op jit(solution)/shard_map/cold_to_owner/pallas_call | solution.py:480
  359.7 72.2 %exchange.3 = f32[32,1,128]{2,1,0:T(1,128)} custom-call(f32[32,1,128]{2,1,0:T(1,128)} %pad.16.refs_0_), custom_call_target="tpu_custom_call" | custom-call | tf_op jit(solution)/shard_map/exchange/pallas_call | solution.py:387
  431.9 1.3 reduce_sum.117
  433.2 0.7 collective-permute-start.5
  435.1 7.2 fusion.29
  442.3 7.0 fusion.33
  449.4 7.1 fusion.37
  456.4 5.4 fusion.22
  461.8 251.1 %reduce_blocks.1 = (f32[1,1,1,64,2048]{4,3,2,1,0:T(8,128)}, f32[1,1,1,64,2048]{4,3,2,1,0:T(8,128)}, f32[1,1,1,64,2048]{4,3,2,1,0:T(8,128)}, f32[4,2,2,64,2048]{4,3,2,1,0:T(8,128)}) custom-call(f32[4,2,2,128,1024]{4,3,2,1,0:T(8,128)} %bitcast.147, f32[4,2,2,128,1024]{4,3,2,1,0:T(8,128)} %bitcast.148, f32[4,2,2,128,1024]{4,3,2,1,0:T(8,128)} %bitcast.149, ...), custom_call_target="tpu_custom_call" | custom-call | tf_op jit(solution)/shard_map/reduce_blocks/pallas_call | solution.py:340
  712.9 3.4 copy-done.1
  716.3 18.9 %add_rows.2 = f32[1000,2048]{1,0:T(8,128)} custom-call(s32[32,256]{1,0:T(8,128)S(1)} %bitcast.155, s32[32]{0:T(128)S(1)} %get-tuple-element.596, s32[32]{0:T(128)S(1)} %get-tuple-element.308.count, s32[1]{0:T(128)} %bitcast.22.base, f32[1024,2048]{1,0:T(8,128)S(1)} %bitcast.137, f32[32,4,8,2048]{3,2,1,0:T(8,128)} %cold_to_owner.2.rows), custom_call_target="tpu_custom_call" | custom-call | tf_op jit(solution)/shard_map/add_rows/pallas_call | solution.py:539
  735.2 2.0 copy.60
  737.2 0.8 copy.61
  738.0 0.8 copy.62
  (91 shorter events, 6.7 us)
Async XLA Ops:
  2.9 432.2 %collective-permute-start.1 = (bf16[256,1024]{1,0:T(8,128)(2,1)}, bf16[256,1024]{1,0:T(8,128)(2,1)}, u32[]{:S(2)}, u32[]{:S(2)}) collective-permute-start(bf16[256,1024]{1,0:T(8,128)(2,1)} %get-tuple-element.328), channel_id=1, source_target_pairs={{0,1},{1,0},{2,3},{3,2},{4,5},{5,4},{6,7},{7,6},{8,9},{9,8},{10,11... | collective-permute-start | bytes 1572872 | tf_op jit(solution)/shard_map/ppermute | solution.py:614
  2.9 430.3 %collective-permute-start.4 = (s32[256]{0:T(256)}, s32[256]{0:T(256)}, u32[]{:S(2)}, u32[]{:S(2)}) collective-permute-start(s32[256]{0:T(256)} %bitcast.169), channel_id=1, source_target_pairs={{0,1},{1,0},{2,3},{3,2},{4,5},{5,4},{6,7},{7,6},{8,9},{9,8},{10,11... | collective-permute-start | bytes 3080 | tf_op jit(solution)/shard_map/ppermute | solution.py:614
  20.2 5.7 copy-start.2
  32.1 2.7 copy-start.16
  117.9 2.1 copy-start.10
  117.9 2.1 copy-start.11
  253.6 5.0 copy-start.17
  253.6 5.1 copy-start.7
  258.7 5.9 copy-start.8
  258.7 6.1 copy-start.18
  258.7 8.5 %slice-start = ((s8[8388608]{0:T(1024)(128)(4,1)}), s8[4194304]{0:T(1024)(128)(4,1)S(1)}, s32[]{:S(2)}) async-start(s8[8388608]{0:T(1024)(128)(4,1)} %bitcast.183), calls=%async_computation | async-start | bytes 8388608
  264.8 2.4 copy-start.5
  264.8 2.4 copy-start.9
  264.8 3.5 slice-start.1
  264.8 9.9 %slice-start.2 = ((s8[8388608]{0:T(1024)(128)(4,1)}), s8[4194304]{0:T(1024)(128)(4,1)S(1)}, s32[]{:S(2)}) async-start(s8[8388608]{0:T(1024)(128)(4,1)} %bitcast.189), calls=%async_computation.2 | async-start | bytes 8388608
  268.3 6.4 slice-start.3
  271.7 163.3 %collective-permute-start = (bf16[256,2048]{1,0:T(8,128)(2,1)S(1)}, bf16[256,2048]{1,0:T(8,128)(2,1)}, u32[]{:S(2)}, u32[]{:S(2)}) collective-permute-start(bf16[256,2048]{1,0:T(8,128)(2,1)S(1)} %get-tuple-element.320), channel_id=1, source_target_pairs={{0,1},{1,0},{2,3},{3,2},{4,5},{5,4},{6,7},{7,6},{8,9},{9,8},{10,11... | collective-permute-start | bytes 3145736 | tf_op jit(solution)/shard_map/ppermute | solution.py:614
  273.1 169.2 %collective-permute-start.2 = (bf16[256,1024]{1,0:T(8,128)(2,1)}, bf16[256,1024]{1,0:T(8,128)(2,1)}, u32[]{:S(2)}, u32[]{:S(2)}) collective-permute-start(bf16[256,1024]{1,0:T(8,128)(2,1)} %get-tuple-element.326), channel_id=1, source_target_pairs={{0,1},{1,0},{2,3},{3,2},{4,5},{5,4},{6,7},{7,6},{8,9},{9,8},{10,11... | collective-permute-start | bytes 1572872 | tf_op jit(solution)/shard_map/ppermute | solution.py:614
  274.5 174.9 %collective-permute-start.3 = (bf16[256,1024]{1,0:T(8,128)(2,1)}, bf16[256,1024]{1,0:T(8,128)(2,1)}, u32[]{:S(2)}, u32[]{:S(2)}) collective-permute-start(bf16[256,1024]{1,0:T(8,128)(2,1)} %get-tuple-element.324), channel_id=1, source_target_pairs={{0,1},{1,0},{2,3},{3,2},{4,5},{5,4},{6,7},{7,6},{8,9},{9,8},{10,11... | collective-permute-start | bytes 1572872 | tf_op jit(solution)/shard_map/ppermute | solution.py:614
  433.2 23.3 %collective-permute-start.5 = (f32[256,1024]{1,0:T(8,128)}, f32[256,1024]{1,0:T(8,128)S(1)}, u32[]{:S(2)}, u32[]{:S(2)}) collective-permute-start(f32[256,1024]{1,0:T(8,128)} %get-tuple-element.322), channel_id=1, source_target_pairs={{0,1},{1,0},{2,3},{3,2},{4,5},{5,4},{6,7},{7,6},{8,9},{9,8},{10,11... | collective-permute-start | bytes 3145736 | tf_op jit(solution)/shard_map/ppermute | solution.py:614
  435.1 7.2 copy-start.15
  442.3 7.1 copy-start.14
  449.4 7.1 copy-start.6
  461.8 251.1 %copy-start.3 = (s32[4,8,2,128]{3,1,2,0:T(8,128)S(1)}, s32[4,8,2,128]{3,1,2,0:T(8,128)}, u32[]{:S(2)}) copy-start(s32[4,8,2,128]{3,1,2,0:T(8,128)} %copy-done.2) | copy-start | bytes 98308
  712.9 3.4 copy-start.1
  716.3 18.9 %copy-start.4 = (s32[4,8,2,128]{3,1,2,0:T(8,128)S(1)}, s32[4,8,2,128]{3,1,2,0:T(8,128)}, u32[]{:S(2)}) copy-start(s32[4,8,2,128]{3,1,2,0:T(8,128)} %copy-done.2) | copy-start | bytes 98308
  735.2 2.0 copy-start.13
  735.2 2.8 copy-start.12

commit v3 on v2

--- a/solution.py
+++ b/solution.py
@@ -183,8 +183,11 @@
 
 
 def reduce_kernel(parts, first_hops, events, n_arr, rows, collect, *refs):
-    ins, outs = refs[:n_arr], refs[n_arr:2 * n_arr]
-    rest = refs[2 * n_arr:]
+    ins, outs = refs[:n_arr], refs[n_arr + 1:2 * n_arr + 1]
+    cold_src, cold_dst = refs[n_arr], refs[2 * n_arr + 1]
+    cold_ssem, cold_rsem, cold_lsem = refs[-3:]
+    cold_start, cold_finish = cold_copies(True, cold_src, cold_dst, cold_ssem, cold_rsem)
+    rest = refs[2 * n_arr + 2:-3]
     n_part = len(parts)
     recv = []
     at = 0
@@ -294,7 +297,10 @@
         remote(theirs, dst, tsem.at[i], usem.at[i], neighbour("c")).wait()
         pltpu.make_async_copy(mine, dst, osem.at[i]).wait()
 
-    for i, k in events:
+    for turn, (i, k) in enumerate(events):
+        if turn == COLD_TURN:
+            lax.fori_loop(1, NUM_DEV, cold_start, 0)
+            pltpu.make_async_copy(cold_src.at[pl.ds(me, 1)], cold_dst.at[pl.ds(me, 1)], cold_lsem).start()
         dim, ring, _ = steps[i][k]
         start = k - ring
         hop(i, k).wait_recv()
@@ -312,9 +318,11 @@
         for k in range(5):
             hop(i, k).wait_send()
         finish_wait(i)
-
-
-def reduce_scatter_blocks(arrays, plan, collect, collective_id):
+    lax.fori_loop(1, NUM_DEV, cold_finish, 0)
+    pltpu.make_async_copy(cold_src.at[pl.ds(me, 1)], cold_dst.at[pl.ds(me, 1)], cold_lsem).wait()
+
+
+def reduce_scatter_blocks(arrays, cold, plan, collect, collective_id):
     parts, first, events = plan
     n = len(arrays)
     rows = [a.shape[0] // 16 for a in arrays]
@@ -337,16 +345,18 @@
             out_shape.append(jax.ShapeDtypeStruct((1, 1, 1, rows[i] // 2, 2 * a.shape[1]), jnp.float32))
     if collect:
         scratch.append(pltpu.SemaphoreType.DMA((m, NUM_DEV)))
+    scratch += [pltpu.SemaphoreType.DMA((NUM_DEV,)), pltpu.SemaphoreType.DMA((NUM_DEV,)), pltpu.SemaphoreType.DMA]
+    out_shape.append(jax.ShapeDtypeStruct(cold.shape, cold.dtype))
     outs = pl.pallas_call(
         functools.partial(reduce_kernel, parts, first, events, n, rows, {i: arrays[i].shape[1] for i in collect}),
         out_shape=out_shape,
-        in_specs=[pl.BlockSpec(memory_space=pl.ANY)] * n,
-        out_specs=[pl.BlockSpec(memory_space=pl.ANY)] * n,
+        in_specs=[pl.BlockSpec(memory_space=pl.ANY)] * (n + 1),
+        out_specs=[pl.BlockSpec(memory_space=pl.ANY)] * (n + 1),
         scratch_shapes=scratch,
         compiler_params=pltpu.CompilerParams(collective_id=collective_id, has_side_effects=True, vmem_limit_bytes=60 * 2**20),
         name="reduce_blocks",
-    )(*ins)
-    return [o.reshape(-1, o.shape[-1]) for o in outs]
+    )(*ins, cold)
+    return [o.reshape(-1, o.shape[-1]) for o in outs[:-1]] + [outs[-1]]
 
 
 def exchange_kernel(n_arr, *refs):
@@ -407,6 +417,33 @@
     return blocks
 
 
+def cold_copies(to_owner, src, dst, ssem, rsem):
+    me = lax.axis_index(AXIS_NAME)
+
+    def copy(step, n):
+        to = (me + step) % NUM_DEV
+        return remote(src.at[pl.ds(to, 1), pl.ds(0, n)], dst.at[pl.ds(me, 1), pl.ds(0, n)], ssem.at[step], rsem.at[step], to)
+
+    def by_size(owner, do):
+        wide = owner < 0
+        for first, last, n in WIDE_OWNERS:
+            hit = (owner >= first) & (owner < last)
+            wide = wide | hit
+            pl.when(hit)(functools.partial(do, n))
+        pl.when(jnp.logical_not(wide))(functools.partial(do, 1))
+
+    def start(step, carry):
+        by_size((me + step) % NUM_DEV if to_owner else me, lambda n: copy(step, n).start())
+        return carry
+
+    def finish(step, carry):
+        by_size((me + step) % NUM_DEV if to_owner else me, lambda n: copy(step, n).wait_send())
+        by_size(me if to_owner else (me - step + NUM_DEV) % NUM_DEV, lambda n: copy(step, n).wait_recv())
+        return carry
+
+    return start, finish
+
+
 def cold_kernel(to_owner, *refs):
     if to_owner:
         src, dst, ssem, rsem, lsem = refs
@@ -415,29 +452,10 @@
     me = lax.axis_index(AXIS_NAME)
     entry_barrier()
 
-    def copy(step, n):
-        to = (me + step) % NUM_DEV
-        return remote(src.at[pl.ds(to, 1), pl.ds(0, n)], dst.at[pl.ds(me, 1), pl.ds(0, n)], ssem.at[step], rsem.at[step], to)
+    start, finish = cold_copies(to_owner, src, dst, ssem, rsem)
 
     def hand(to):
         return remote(rows.at[pl.ds(to, 1)], row_dst, hsem.at[to], gsem.at[0], to)
-
-    def by_size(owner, do):
-        wide = owner < 0
-        for first, last, n in WIDE_OWNERS:
-            hit = (owner >= first) & (owner < last)
-            wide = wide | hit
-            pl.when(hit)(functools.partial(do, n))
-        pl.when(jnp.logical_not(wide))(functools.partial(do, 1))
-
-    def start(step, carry):
-        by_size((me + step) % NUM_DEV if to_owner else me, lambda n: copy(step, n).start())
-        return carry
-
-    def finish(step, carry):
-        by_size((me + step) % NUM_DEV if to_owner else me, lambda n: copy(step, n).wait_send())
-        by_size(me if to_owner else (me - step + NUM_DEV) % NUM_DEV, lambda n: copy(step, n).wait_recv())
-        return carry
 
     def each(do):
         def body(to, carry):
@@ -589,6 +607,7 @@
      (2, 2, 'xyz')),
     "adefhbigcjk", "gabjgdcijgecikadjgcfiadeciadeafdhefbefhbkfhbjkghcibjkhk")
 HOT_ROWS = 1024
+COLD_TURN = 27
 
 
 def norm_forward(x_rows, gain_full):
@@ -685,21 +704,26 @@
         pair_ids = jnp.concatenate([tok, partner(tok)])
         pair_sel = ((pair_ids[:, None] == jnp.arange(HOT_ROWS, dtype=jnp.int32)) & (pair_ids[:, None] < vocab_local)).astype(jnp.float32)
         hot_part = dot(pair_sel, paired(d_x), ((0,), (0,)), lax.Precision.HIGHEST)
-        d_w_query, d_w_key, d_w_value, hot_sum = reduce_scatter_blocks([*d_w, hot_part], REDUCE_PLAN, (3,), 2)
+        def owner_rows(step):
+            want = my_first[:, None] + step * caps[:, None] + slot
+            src = jnp.sum(jnp.where(want[:, :, None] == rank, pos, 0), axis=2)
+            return jnp.take(d_x, src.reshape(-1), axis=0).reshape(NUM_DEV, MOST, BLOCK, width)
+
+        def add_round(step, total, got, fresh):
+            left = jnp.clip(owner_count - step * my_cap, 0, my_cap)
+            return add_rows(fresh, vocab_local, ids_all, owner_first + step * my_cap, left, base, total, got)
+
+        d_w_query, d_w_key, d_w_value, hot_sum, cold_got = reduce_scatter_blocks(
+            [*d_w, hot_part], owner_rows(0), REDUCE_PLAN, (3,), 2)
 
         gain_blocks = jnp.pad(gain_part.reshape(NUM_DEV, 1, -1), ((0, 0), (0, 0), (0, 128 - gain_rows)))
         d_norm_gain = jnp.sum(exchange([gain_blocks], 5)[0], axis=(0, 1))[:gain_rows]
-        def add_round(step, total, fresh):
-            want = my_first[:, None] + step * caps[:, None] + slot
-            src = jnp.sum(jnp.where(want[:, :, None] == rank, pos, 0), axis=2)
-            rows = jnp.take(d_x, src.reshape(-1), axis=0).reshape(NUM_DEV, MOST, BLOCK, width)
-            got = cold_exchange([rows], 7)[0]
-            left = jnp.clip(owner_count - step * my_cap, 0, my_cap)
-            return add_rows(fresh, vocab_local, ids_all, owner_first + step * my_cap, left, base, total, got)
-
-        _, d_embed = lax.while_loop(lambda carry: carry[0] < rounds,
-                                    lambda carry: (carry[0] + 1, add_round(*carry, False)),
-                                    (jnp.int32(1), add_round(jnp.int32(0), hot_sum, True)))
+        def more_rows(carry):
+            step, total = carry
+            return step + 1, add_round(step, total, cold_exchange([owner_rows(step)], 7)[0], False)
+
+        _, d_embed = lax.while_loop(lambda carry: carry[0] < rounds, more_rows,
+                                    (jnp.int32(1), add_round(jnp.int32(0), hot_sum, cold_got, True)))
         return (query_proj, key_proj, value_proj, d_embed, d_norm_gain, d_w_query, d_w_key, d_w_value)
 
     row_spec = P(AXIS_NAME, None)

time: 746 us -> 724 us (0.971)
  the two profiles are of different devices: /device:TPU:1 before, /device:TPU:14 now
where the time goes in v3:
time: 724 us; the launch traced here: 709 us
  Pallas kernels  583 us (81%)
  matrix products  68.4 us (9%)
  local copies, waits for them, and re-layouts  31.8 us (4%)
  other arithmetic  23.2 us (3%)
    pallas_call x1, Pallas kernels, reduce_scatter_blocks(): pl.pallas_call(functools.partial(reduce_kernel, parts, first, events, n,...  349 us
    pallas_call x1, Pallas kernels, all_gather_blocks(): pl.pallas_call(functools.partial(gather_kernel, parts, first, events, n),...  164 us
    dot_general x12, matrix products, dot(): lax.dot_general(a, b, (dims, ((), ())), preferred_element_type=jnp.float3...  68.4 us
    pallas_call x1, Pallas kernels, cold_exchange(): pl.pallas_call(functools.partial(cold_kernel, to_owner), out_shape=out_sh...  42.9 us
    pallas_call x2, Pallas kernels, exchange(): pl.pallas_call(functools.partial(exchange_kernel, n), out_shape=[jax.Shap...  18.6 us
  transfers between devices with their start and end apart: 6, of which 0 were waited for; matrix products, arithmetic and copies ran while one was open for 16% of the time, Pallas kernels for 32%

profile of v3, /device:TPU:14, one launch (start us, length us, event | category | flops | bytes accessed | tf_op | source)
XLA Modules:
  0.0 709.4 jit_solution(7272613000609357765)
XLA Ops:
  0.8 2.3 dynamic-slice_bitcast_fusion.5
  3.5 2.3 dynamic-slice_bitcast_fusion.3
  5.9 1.1 dynamic-slice_bitcast_fusion.1
  7.3 0.6 compare_reduce_fusion
  8.3 0.6 broadcast_in_dim.203.refs_1_
  8.9 0.6 broadcast_in_dim.202.refs_0_
  9.6 9.2 %exchange.2 = (s32[32,2,128]{2,1,0:T(2,128)S(1)}, f32[32,1,128]{2,1,0:T(1,128)}) custom-call(s32[32,2,128]{2,1,0:T(2,128)} %broadcast_in_dim.202.refs_0_, f32[32,1,128]{2,1,0:T(1,128)} %broadcast_in_dim.203.refs_1_), custom_call_target="tpu_custom_call" | custom-call | tf_op jit(solution)/shard_map/exchange/pallas_call | solution.py:397
  18.7 0.8 slice_reduce_fusion
  19.6 0.7 convert_reduce_fusion
  20.5 0.7 broadcast_select_fusion.2
  21.2 0.9 fusion.53
  23.0 0.8 select_reduce_fusion.2
  23.9 0.7 convert_bitcast_fusion.2.refs_0_
  24.6 4.0 convert_element_type.54
  28.6 6.2 fusion.17
  34.8 2.5 pad.15
  37.2 42.9 %cold_to_device.2 = (bf16[32,4,8,2048]{3,2,1,0:T(8,128)(2,1)}, bf16[1,32,2048]{2,1,0:T(8,128)(2,1)}) custom-call(bf16[32,4,8,2048]{3,2,1,0:T(8,128)(2,1)} %bitcast.151, bf16[32,32,2048]{2,1,0:T(8,128)(2,1)} %bitcast.140), custom_call_target="tpu_custom_call" | custom-call | tf_op jit(solution)/shard_map/cold_to_device/pallas_call | solution.py:498
  80.1 5.1 gather_fusion.2
  85.6 2.1 convert_bitcast_fusion
  87.7 163.5 %gather_blocks.1 = (bf16[4,2,2,2,64,2048]{5,4,3,2,1,0:T(8,128)(2,1)}, bf16[4,2,2,2,64,2048]{5,4,3,2,1,0:T(8,128)(2,1)}, bf16[4,2,2,2,64,2048]{5,4,3,2,1,0:T(8,128)(2,1)}, bf16[4,2,2,2,32,2048]{5,4,3,2,1,0:T(8,128)(2,1)}) custom-call(bf16[1,1,1,1,64,2048]{5,4,3,2,1,0:T(8,128)(2,1)} %convert_bitcast_fusion.2.refs_0_, ...), custom_call_target="tpu_custom_call" | custom-call | tf_op jit(solution)/shard_map/gather_blocks/pallas_call | solution.py:138
  251.2 3.8 multiply_reduce_fusion.2
  255.0 6.0 fusion.43
  261.1 2.4 convolution_add_fusion.1
  263.5 2.8 multiply_reduce_fusion
  266.4 0.6 subtract_multiply_fusion
  267.4 0.8 select_reduce_fusion.1
  268.3 7.1 %fusion.21 = bf16[1,256,2048]{2,1,0:T(8,128)(2,1)} fusion(bf16[256,2048]{1,0:T(8,128)(2,1)S(1)} %get-tuple-element.322, bf16[2048,2048]{1,0:T(8,128)(2,1)} %bitcast.188), kind=kOutput, calls=%fused_computation.57 | convolution fusion | flops 2148007936 | bytes 10485760 | tf_op jit(solution)/shard_map/dot_general | solution.py:620
  275.4 6.7 fusion.20
  282.3 6.8 gather_fusion.3
  289.1 7.2 %broadcast_select_fusion.1.refs_4_ = f32[32,4,8,2048]{3,2,1,0:T(8,128)} fusion(f32[32,4,8,2048]{3,2,1,0:T(8,128)} %bitcast.145, pred[32,4,8]{2,1,0:T(4,128)(4,1)S(1)} %copy.26), kind=kLoop, calls=%fused_computation.44 | loop fusion | flops 2097152 | bytes 16778240 | tf_op jit(solution)/shard_map/jit(_take)/select_n | solution.py:710
  296.3 6.7 fusion.19
  303.0 1.5 constant_dynamic-slice_fusion.1
  304.5 0.7 maximum_minimum_fusion.1
  305.3 0.6 pad.16.refs_0_
  305.9 9.5 %exchange.3 = f32[32,1,128]{2,1,0:T(1,128)} custom-call(f32[32,1,128]{2,1,0:T(1,128)} %pad.16.refs_0_), custom_call_target="tpu_custom_call" | custom-call | tf_op jit(solution)/shard_map/exchange/pallas_call | solution.py:397
  315.3 1.3 reduce_sum.117
  316.6 0.7 pad_add_fusion
  317.3 0.7 broadcast_compare_fusion.1
  318.0 7.2 %fusion.33 = f32[2048,1024]{1,0:T(8,128)} fusion(bf16[256,1024]{1,0:T(8,128)(2,1)} %collective-permute-done.2, bf16[256,1024]{1,0:T(8,128)(2,1)} %get-tuple-element.327, bf16[256,2048]{1,0:T(8,128)(2,1)} %collective-permute-done, bf16[256,2048]{1,0:T(8,128)(2,1)S(1)} %get-tuple-element.322), kind=kOutput, calls=%fused_computation.76 | convolution fusion | flops 2153775104 | bytes 11534336 | tf_op jit(solution)/shard_map/dot_general | solution.py:620
  325.2 7.0 fusion.37
  332.3 7.1 fusion.29
  339.3 5.4 fusion.22
  344.7 348.6 %reduce_blocks.1 = (f32[1,1,1,64,2048]{4,3,2,1,0:T(8,128)}, f32[1,1,1,64,2048]{4,3,2,1,0:T(8,128)}, f32[1,1,1,64,2048]{4,3,2,1,0:T(8,128)}, f32[4,2,2,64,2048]{4,3,2,1,0:T(8,128)}, f32[32,4,8,2048]{3,2,1,0:T(8,128)}) custom-call(f32[4,2,2,128,1024]{4,3,2,1,0:T(8,128)} %bitcast.149, f32[4,2,2,128,1024]{4,3,2,1,0:T(8,128)} %bitcast.147, ...), custom_call_target="tpu_custom_call" | custom-call | tf_op jit(solution)/shard_map/reduce_blocks/pallas_call | solution.py:350
  693.3 3.4 copy-done.1
  696.7 8.9 %add_rows.2 = f32[1000,2048]{1,0:T(8,128)} custom-call(s32[32,256]{1,0:T(8,128)S(1)} %bitcast.155, s32[32]{0:T(128)S(1)} %get-tuple-element.598, s32[32]{0:T(128)S(1)} %get-tuple-element.310.count, s32[1]{0:T(128)} %bitcast.22.base, f32[1024,2048]{1,0:T(8,128)S(1)} %bitcast.137, f32[32,4,8,2048]{3,2,1,0:T(8,128)} %get-tuple-element.197.rows), custom_call_target="tpu_custom_call" | custom-call | tf_op jit(solution)/shard_map/add_rows/pallas_call | solution.py:557
  705.7 2.0 copy.60
  707.6 0.8 copy.61
  708.4 0.8 copy.62
  (86 shorter events, 3.2 us)
Async XLA Ops:
  0.6 7.3 %copy-start.15 = (s32[1,256]{1,0:T(1,128)S(1)}, s32[1,256]{1,0:T(1,128)}, u32[]{:S(2)}) copy-start(s32[1,256]{1,0:T(1,128)} %param.15) | copy-start | bytes 3076
  0.6 5.2 copy-start.8
  0.7 7.7 %copy-start.16 = (f32[64]{0:T(128)S(1)}, f32[64]{0:T(128)}, u32[]{:S(2)}) copy-start(f32[64]{0:T(128)} %param.17) | copy-start | bytes 772
  0.7 23.2 %copy-start.9 = (f32[64,2048]{1,0:T(8,128)S(1)}, f32[64,2048]{1,0:T(8,128)}, u32[]{:S(2)}) copy-start(f32[64,2048]{1,0:T(8,128)} %param.18) | copy-start | bytes 1572868
  0.7 316.0 %collective-permute-start.4 = (s32[256]{0:T(256)}, s32[256]{0:T(256)}, u32[]{:S(2)}, u32[]{:S(2)}) collective-permute-start(s32[256]{0:T(256)} %bitcast.169), channel_id=1, source_target_pairs={{0,1},{1,0},{2,3},{3,2},{4,5},{5,4},{6,7},{7,6},{8,9},{9,8},{10,11... | collective-permute-start | bytes 3080 | tf_op jit(solution)/shard_map/ppermute | solution.py:633
  3.1 329.1 %collective-permute-start.1 = (bf16[256,1024]{1,0:T(8,128)(2,1)}, bf16[256,1024]{1,0:T(8,128)(2,1)}, u32[]{:S(2)}, u32[]{:S(2)}) collective-permute-start(bf16[256,1024]{1,0:T(8,128)(2,1)} %get-tuple-element.330), channel_id=1, source_target_pairs={{0,1},{1,0},{2,3},{3,2},{4,5},{5,4},{6,7},{7,6},{8,9},{9,8},{10,11... | collective-permute-start | bytes 1572872 | tf_op jit(solution)/shard_map/ppermute | solution.py:633
  5.7 312.2 %collective-permute-start.2 = (bf16[256,1024]{1,0:T(8,128)(2,1)}, bf16[256,1024]{1,0:T(8,128)(2,1)}, u32[]{:S(2)}, u32[]{:S(2)}) collective-permute-start(bf16[256,1024]{1,0:T(8,128)(2,1)} %get-tuple-element.328), channel_id=1, source_target_pairs={{0,1},{1,0},{2,3},{3,2},{4,5},{5,4},{6,7},{7,6},{8,9},{9,8},{10,11... | collective-permute-start | bytes 1572872 | tf_op jit(solution)/shard_map/ppermute | solution.py:633
  6.9 318.3 %collective-permute-start.3 = (bf16[256,1024]{1,0:T(8,128)(2,1)}, bf16[256,1024]{1,0:T(8,128)(2,1)}, u32[]{:S(2)}, u32[]{:S(2)}) collective-permute-start(bf16[256,1024]{1,0:T(8,128)(2,1)} %get-tuple-element.326), channel_id=1, source_target_pairs={{0,1},{1,0},{2,3},{3,2},{4,5},{5,4},{6,7},{7,6},{8,9},{9,8},{10,11... | collective-permute-start | bytes 1572872 | tf_op jit(solution)/shard_map/ppermute | solution.py:633
  19.6 9.0 %copy-start.2 = (s32[4,8,2,128]{3,1,2,0:T(8,128)}, s32[4,8,2,128]{3,1,2,0:T(8,128)S(1)}, u32[]{:S(2)}) copy-start(s32[4,8,2,128]{3,1,2,0:T(8,128)S(1)} %copy.32) | copy-start | bytes 98308
  21.2 1.6 copy-start.14
  251.2 3.8 copy-start.6
  251.2 9.9 %slice-start = ((s8[8388608]{0:T(1024)(128)(4,1)}), s8[4194304]{0:T(1024)(128)(4,1)S(1)}, s32[]{:S(2)}) async-start(s8[8388608]{0:T(1024)(128)(4,1)} %bitcast.185), calls=%async_computation | async-start | bytes 8388608
  255.0 6.1 copy-start.7
  255.0 6.1 slice-start.1
  255.0 8.5 %slice-start.2 = ((s8[8388608]{0:T(1024)(128)(4,1)}), s8[4194304]{0:T(1024)(128)(4,1)S(1)}, s32[]{:S(2)}) async-start(s8[8388608]{0:T(1024)(128)(4,1)} %bitcast.189), calls=%async_computation.2 | async-start | bytes 8388608
  261.1 2.4 slice-start.3
  266.9 51.1 %collective-permute-start = (bf16[256,2048]{1,0:T(8,128)(2,1)S(1)}, bf16[256,2048]{1,0:T(8,128)(2,1)}, u32[]{:S(2)}, u32[]{:S(2)}) collective-permute-start(bf16[256,2048]{1,0:T(8,128)(2,1)S(1)} %get-tuple-element.322), channel_id=1, source_target_pairs={{0,1},{1,0},{2,3},{3,2},{4,5},{5,4},{6,7},{7,6},{8,9},{9,8},{10,11... | collective-permute-start | bytes 3145736 | tf_op jit(solution)/shard_map/ppermute | solution.py:633
  316.6 22.7 %collective-permute-start.5 = (f32[256,1024]{1,0:T(8,128)}, f32[256,1024]{1,0:T(8,128)S(1)}, u32[]{:S(2)}, u32[]{:S(2)}) collective-permute-start(f32[256,1024]{1,0:T(8,128)} %get-tuple-element.324), channel_id=1, source_target_pairs={{0,1},{1,0},{2,3},{3,2},{4,5},{5,4},{6,7},{7,6},{8,9},{9,8},{10,11... | collective-permute-start | bytes 3145736 | tf_op jit(solution)/shard_map/ppermute | solution.py:633
  318.0 7.2 %copy-start.13 = (bf16[256,1024]{1,0:T(8,128)(2,1)S(1)}, bf16[256,1024]{1,0:T(8,128)(2,1)}, u32[]{:S(2)}) copy-start(bf16[256,1024]{1,0:T(8,128)(2,1)} %get-tuple-element.325) | copy-start | bytes 1572868
  325.2 7.0 copy-start.12
  332.3 7.1 copy-start.5
  344.7 348.6 %copy-start.3 = (s32[4,8,2,128]{3,1,2,0:T(8,128)S(1)}, s32[4,8,2,128]{3,1,2,0:T(8,128)}, u32[]{:S(2)}) copy-start(s32[4,8,2,128]{3,1,2,0:T(8,128)} %copy-done.2) | copy-start | bytes 98308
  693.3 3.4 copy-start.1
  696.7 9.0 %copy-start.4 = (s32[4,8,2,128]{3,1,2,0:T(8,128)S(1)}, s32[4,8,2,128]{3,1,2,0:T(8,128)}, u32[]{:S(2)}) copy-start(s32[4,8,2,128]{3,1,2,0:T(8,128)} %copy-done.2) | copy-start | bytes 98308
  705.6 2.0 copy-start.11
  705.7 2.8 copy-start.10
